TPU v7x, 512 devices: a whole 4x8x8 slice. The times are simulated.
512 devices in a mesh: sp: 64 (over y, x, core), pb: 8 (over z).
Axes of the slice: x: 4, y: 8, z: 8, core: 2. Of those that a mesh axis runs over, the one named last changes fastest.
Arguments:
- amplitudes: bfloat16 [160, 1024, 1024], P('pb', 'sp'), may hold values from -6 to 6
- virtuals: bfloat16 [1400, 1024], replicated, may hold values from -0.375 to 0.375
- energies: float32 [1024], replicated, may hold values from 0.02 to 0.2
- integrals: bfloat16 [8192, 2048], P('sp'), may hold values from -0.125 to 0.125
- screened: int32 [64, 16], P('sp'), may hold values from 0 to 63, as said below
- counts: int32 [64], P('sp'), may hold values from 1 to 16, 512 in all
- offsets: int32 [2, 64], replicated, may hold values from 0 to 1384
- coupling: bfloat16 [160, 160], P('pb'), may hold values from -0.5 to 0.5
Outputs:
- residual: bfloat16 [160, 1024, 1024], P('pb', 'sp')
Inputs may be any that keep to these rules, and one draw needn't show every extreme that they name: `screened`: each row names 16 different blocks.
All inputs are finite; a program needn't handle non-finite values. No bound on the sum of `counts` on one device may be relied on, other than what follows from the above.
Results may differ from a plain program's by a relative error of at most 0.01.
Values may be sent and summed in bfloat16 or wider, within the bound.
A program may use at most 64 MiB of HBM per device.

v0:
```python
import jax
import jax.numpy as jnp
from jax import lax
from jax.sharding import PartitionSpec as P

SHELL_ROW = 8
SHELL_COL = 16


def split_up(shard, dim, size):
    lengths = shard.shape
    tiles = shard.reshape(*lengths[:dim], size, lengths[dim] // size, *lengths[dim + 1 :])
    return jnp.moveaxis(tiles, dim, 0)


def summed_on_arrival(shard, axis, dim):
    size = lax.axis_size(axis)
    tiles = lax.all_to_all(split_up(shard, dim, size), axis, 0, 0, tiled=True)
    return jnp.sum(tiles, axis=0)


def laid_out(tiles, dim):
    lengths = list(tiles.shape[1:])
    lengths[dim] *= tiles.shape[0]
    return jnp.moveaxis(tiles, 0, dim).reshape(lengths)


def copy_for_each(shard, axis):
    size = lax.axis_size(axis)
    return lax.all_to_all(
        jnp.broadcast_to(shard[None], (size, *shard.shape)), axis, 0, 0, tiled=True
    )


def gather_directly(shard, axis, dim):
    return laid_out(copy_for_each(shard, axis), dim)


def shards(amplitudes, virtuals, energies, integrals, screened, counts, offsets, coupling):
    pairs = amplitudes.shape[0]
    ext_rows = amplitudes.shape[1]
    width = SHELL_ROW * SHELL_COL
    nblk = lax.axis_size("sp")
    first = lax.axis_index("sp") * ext_rows
    local_cols = lax.dynamic_slice_in_dim(virtuals, first, ext_rows, 1)
    half = jnp.einsum(
        "pab,nb->pan", amplitudes, virtuals, preferred_element_type=jnp.float32
    ).astype(jnp.bfloat16)
    row_span = jnp.arange(SHELL_ROW, dtype=jnp.int32)
    col_span = jnp.arange(SHELL_COL, dtype=jnp.int32)
    lows = offsets[0]
    highs = offsets[1]
    left = local_cols[lows[:, None] + row_span[None, :]]
    right = half[:, :, highs[:, None] + col_span[None, :]]
    term = jnp.einsum("bia,pabs->bpis", left, right, preferred_element_type=jnp.float32)
    mine = summed_on_arrival(term.reshape(1 * lax.axis_size("sp"), pairs, width), "sp", 0).astype(
        jnp.bfloat16
    )
    ao_all = gather_directly(mine, "sp", 0)
    slots = screened.shape[1]
    live = (jnp.arange(slots, dtype=jnp.int32) < counts[0]).astype(jnp.bfloat16)
    chosen = jnp.take(ao_all, screened[0], axis=0) * live[:, None, None]
    slab = integrals.reshape(width, slots, width)
    raw = jnp.einsum("rkc,kpc->pr", slab, chosen, preferred_element_type=jnp.float32).astype(
        jnp.bfloat16
    )
    batch = gather_directly(raw[None], "pb", 1)
    mixed = jnp.einsum("pq,bqc->bpc", coupling, batch, preferred_element_type=jnp.float32).astype(
        jnp.bfloat16
    )
    k_all = gather_directly(mixed, "sp", 0)
    left_all = local_cols[offsets[0][:, None] + row_span[None, :]]
    right_rows = virtuals[offsets[1][:, None] + col_span[None, :]]
    square = k_all.reshape(nblk, pairs, SHELL_ROW, SHELL_COL)
    upper = jnp.einsum(
        "bia,bpis->pabs", left_all, square, preferred_element_type=jnp.float32
    ).astype(jnp.bfloat16)
    inner = jnp.einsum("pabs,bsn->pan", upper, right_rows, preferred_element_type=jnp.float32)
    own_energy = lax.dynamic_slice_in_dim(energies, first, ext_rows)
    diag = own_energy[:, None] + energies[None, :]
    return (inner + diag[None] * amplitudes.astype(jnp.float32)).astype(jnp.bfloat16)


def solution(mesh):
    return jax.shard_map(
        shards,
        mesh=mesh,
        in_specs=(
            P("pb", "sp", None),
            P(),
            P(),
            P("sp", None),
            P("sp", None),
            P("sp"),
            P(),
            P("pb", None),
        ),
        out_specs=P("pb", "sp", None),
        check_vma=False,
    )
```

profile of v0, /device:TPU:1, one launch (start us, length us, event | category | flops | bytes accessed | tf_op | source)
XLA Modules:
  0.0 165.5 jit_solution(4012213103695011373)
XLA Ops:
  0.0 0.0 copy-start
  0.0 1.8 %copy-done = bf16[1400,1024]{1,0:T(8,128)(2,1)S(1)} copy-done((bf16[1400,1024]{1,0:T(8,128)(2,1)S(1)}, bf16[1400,1024]{1,0:T(8,128)(2,1)}, u32[]{:S(2)}) %copy-start) | copy-done | bytes 2867224
  1.8 3.3 %fusion.2 = bf16[20,16,1400]{2,1,0:T(8,128)(2,1)} fusion(bf16[20,16,1024]{2,1,0:T(8,128)(2,1)} %param.8, bf16[1400,1024]{1,0:T(8,128)(2,1)S(1)} %copy-done), kind=kOutput, calls=%fused_computation.7 | convolution fusion | flops 917952000 | bytes 4418560 | tf_op jit(solution)/shard_map/pab,nb->pan/dot_general | solution.py:46
  5.1 0.0 copy-start.5
  5.1 7.9 %copy.18 = bf16[20,16,1400]{0,1,2:T(8,128)(2,1)} copy(bf16[20,16,1400]{2,1,0:T(8,128)(2,1)} %fusion.2) | data formatting | bytes 1792000 | tf_op jit(solution)/shard_map/convert_element_type | solution.py:48
  13.0 0.0 copy-done.5
  13.0 0.1 compare_select_fusion.1
  13.1 0.1 reshape.184
  13.2 0.2 constant_dynamic-slice_fusion
  13.4 0.1 compare_select_fusion
  13.4 0.1 reshape.192
  13.5 11.1 %gather_fusion = bf16[1024,20,16]{1,2,0:T(8,128)(2,1)} fusion(bf16[20,16,1400]{0,1,2:T(8,128)(2,1)} %copy.18, s32[1024]{0:T(1024)S(1)} %broadcast_clamp_fusion), kind=kCustom, calls=%fused_computation | custom fusion | bytes 1314816 | tf_op jit(solution)/shard_map/gather | solution.py:54
  24.6 1.3 gather_fusion.1
  26.0 0.0 copy-start.1
  26.0 4.9 %convolution_bitcast_fusion = f32[64,20,8,16]{1,2,3,0:T(8,128)} fusion(bf16[20,16,64,16]{0,1,3,2:T(8,128)(2,1)} %bitcast.75, bf16[512,16]{1,0:T(8,128)(2,1)S(1)} %gather_fusion.1), kind=kOutput, calls=%fused_computation.8 | convolution fusion | flops 5242880 | bytes 1327104 | tf_op jit(solution)/shard_map/bia,pabs->bpis/dot_general | solution.py:55
  30.8 0.0 copy-done.1
  30.8 4.9 %copy.21 = f32[64,20,8,16]{0,3,2,1:T(8,128)} copy(f32[64,20,8,16]{1,2,3,0:T(8,128)} %convolution_bitcast_fusion) | data formatting | bytes 1310720 | tf_op jit(solution)/shard_map/bia,pabs->bpis/transpose | solution.py:55
  35.8 0.0 copy-start.6
  35.8 0.0 copy-start.3
  35.8 3.2 %copy.22 = f32[64,1,20,128]{3,1,2,0:T(1,128)} copy(f32[64,1,20,128]{0,3,2,1:T(8,128)} %bitcast.76) | data formatting | bytes 1310720 | tf_op jit(solution)/shard_map/reshape;reshape | solution.py:12
  39.0 32.0 %all_to_all.20 = f32[64,1,20,128]{3,1,2,0:T(1,128)S(1)} all-to-all(f32[64,1,20,128]{3,1,2,0:T(1,128)} %copy.22), channel_id=1, replica_groups=mesh['sp'=64,'pb'=8] {'sp'}, dimensions={0} | all-to-all | bytes 1310720 | tf_op jit(solution)/shard_map/all_to_all | solution.py:18
  70.9 0.5 reduce_sum.9
  71.4 0.8 broadcast_in_dim.19
  72.2 5.8 %all-to-all-start.1 = ((bf16[64,1,20,128]{3,2,1,0:T(8,128)(2,1)}), bf16[64,1,20,128]{3,2,1,0:T(8,128)(2,1)S(1)}, u32[]{:S(2)}, u32[]{:S(2)}) async-start(bf16[64,1,20,128]{3,2,1,0:T(8,128)(2,1)} %broadcast_in_dim.19), calls=%async_computation.1 | async-start | bytes 786432 | tf_op jit(solution)/shard_map/all_to_all | solution.py:30
  78.6 0.0 copy-done.6
  78.7 14.5 %all-to-all-done.1 = bf16[64,1,20,128]{3,2,1,0:T(8,128)(2,1)S(1)} async-done(((bf16[64,1,20,128]{3,2,1,0:T(8,128)(2,1)}), bf16[64,1,20,128]{3,2,1,0:T(8,128)(2,1)S(1)}, u32[]{:S(2)}, u32[]{:S(2)}) %all-to-all-start.1) | async-done | bytes 327712 | tf_op jit(solution)/shard_map/all_to_all | solution.py:30
  93.2 0.6 gather_fusion.2
  93.7 1.3 fusion.7
  95.1 16.9 %all_to_all.21 = bf16[8,1,20,128]{3,2,1,0:T(8,128)(2,1)S(1)} all-to-all(bf16[8,1,20,128]{3,2,1,0:T(8,128)(2,1)S(1)} %broadcast_in_dim.21), channel_id=1, replica_groups=mesh['sp'=64,'pb'=8] {'pb'}, dimensions={0} | all-to-all | bytes 81920 | tf_op jit(solution)/shard_map/all_to_all | solution.py:30
  112.0 0.0 copy-done.3
  112.0 0.1 fusion.8
  112.1 0.8 broadcast_in_dim.23
  112.9 7.1 %all-to-all-start.3 = ((bf16[64,1,20,128]{3,2,1,0:T(8,128)(2,1)}), bf16[64,1,20,128]{3,2,1,0:T(8,128)(2,1)}, u32[]{:S(2)}, u32[]{:S(2)}) async-start(bf16[64,1,20,128]{3,2,1,0:T(8,128)(2,1)} %broadcast_in_dim.23), calls=%async_computation.3 | async-start | bytes 786432 | tf_op jit(solution)/shard_map/all_to_all | solution.py:30
  120.0 0.0 copy-start.4
  120.0 5.4 %gather_fusion.3 = bf16[1024,1024]{1,0:T(8,128)(2,1)} fusion(bf16[1400,1024]{1,0:T(8,128)(2,1)S(1)} %copy-done, s32[1024]{0:T(1024)S(1)} %broadcast_clamp_fusion), kind=kCustom, calls=%fused_computation.3 | custom fusion | bytes 4198400 | tf_op jit(solution)/shard_map/gather | solution.py:73
  125.4 0.0 copy-done.4
  125.4 0.1 dynamic_slice.7
  125.4 0.7 broadcast_add_fusion
  126.2 8.9 %all-to-all-done.3 = bf16[64,1,20,128]{3,2,1,0:T(8,128)(2,1)} async-done(((bf16[64,1,20,128]{3,2,1,0:T(8,128)(2,1)}), bf16[64,1,20,128]{3,2,1,0:T(8,128)(2,1)}, u32[]{:S(2)}, u32[]{:S(2)}) %all-to-all-start.3) | async-done | bytes 327712 | tf_op jit(solution)/shard_map/all_to_all | solution.py:30
  135.1 1.3 copy.24
  136.4 4.4 %copy.25 = bf16[64,20,8,16]{1,2,3,0:T(8,128)(2,1)} copy(bf16[64,20,8,16]{0,3,2,1:T(8,128)(2,1)S(1)} %bitcast.77) | data formatting | bytes 655360 | tf_op jit(solution)/shard_map/reshape;reshape | solution.py:74
  140.8 4.9 %convert_bitcast_fusion = bf16[20,16,64,16]{0,1,3,2:T(8,128)(2,1)} fusion(bf16[64,20,8,16]{1,2,3,0:T(8,128)(2,1)} %copy.25, bf16[512,16]{1,0:T(8,128)(2,1)} %copy-done.1), kind=kOutput, calls=%fused_computation.4 | convolution fusion | flops 5570560 | bytes 999424 | tf_op jit(solution)/shard_map/bia,bpis->pabs/dot_general | solution.py:75
  145.7 0.0 copy-start.2
  145.7 13.6 %copy.29 = bf16[20,16,64,16]{3,1,2,0:T(8,128)(2,1)} copy(bf16[20,16,64,16]{0,1,3,2:T(8,128)(2,1)} %convert_bitcast_fusion) | data formatting | bytes 1310720 | tf_op jit(solution)/shard_map/convert_element_type | solution.py:77
  159.4 0.0 copy-done.2
  159.4 6.2 %fusion.6 = bf16[20,16,1024]{2,1,0:T(8,128)(2,1)} fusion(bf16[20,16,64,16]{3,1,2,0:T(8,128)(2,1)} %copy.29, bf16[64,16,1024,1]{2,1,0,3:T(8,128)(2,1)} %bitcast.78, bf16[20,16,1024]{2,1,0:T(8,128)(2,1)} %param.8, f32[16,1024]{1,0:T(8,128)S(1)} %copy-done.2), kind=kOutput, calls=%fused_computation.11 | convolution fusion | flops 672399360 | bytes 4128768 | tf_op jit(solution)/shard_map/pabs,bsn->pan/dot_general | solution.py:78
  (8 shorter events, 0.1 us)
Async XLA Ops:
  0.0 1.8 %copy-start = (bf16[1400,1024]{1,0:T(8,128)(2,1)S(1)}, bf16[1400,1024]{1,0:T(8,128)(2,1)}, u32[]{:S(2)}) copy-start(bf16[1400,1024]{1,0:T(8,128)(2,1)} %param.9) | copy-start | bytes 8601604
  5.1 7.9 %copy-start.5 = (s32[2,64]{1,0:T(2,128)S(1)}, s32[2,64]{1,0:T(2,128)}, u32[]{:S(2)}) copy-start(s32[2,64]{1,0:T(2,128)} %param.14) | copy-start | bytes 1540
  26.0 4.9 %copy-start.1 = (bf16[512,16]{1,0:T(8,128)(2,1)}, bf16[512,16]{1,0:T(8,128)(2,1)S(1)}, u32[]{:S(2)}) copy-start(bf16[512,16]{1,0:T(8,128)(2,1)S(1)} %gather_fusion.1) | copy-start | bytes 49156
  35.8 42.9 %copy-start.6 = (s32[1,16]{1,0:T(1,128)S(1)}, s32[1,16]{1,0:T(1,128)}, u32[]{:S(2)}) copy-start(s32[1,16]{1,0:T(1,128)} %param.12) | copy-start | bytes 196
  35.8 76.2 %copy-start.3 = (bf16[20,160]{1,0:T(8,128)(2,1)S(1)}, bf16[20,160]{1,0:T(8,128)(2,1)}, u32[]{:S(2)}) copy-start(bf16[20,160]{1,0:T(8,128)(2,1)} %param.15) | copy-start | bytes 19204
  72.2 21.0 %all-to-all-start.1 = ((bf16[64,1,20,128]{3,2,1,0:T(8,128)(2,1)}), bf16[64,1,20,128]{3,2,1,0:T(8,128)(2,1)S(1)}, u32[]{:S(2)}, u32[]{:S(2)}) async-start(bf16[64,1,20,128]{3,2,1,0:T(8,128)(2,1)} %broadcast_in_dim.19), calls=%async_computation.1 | async-start | bytes 786432 | tf_op jit(solution)/shard_map/all_to_all | solution.py:30
  112.9 22.2 %all-to-all-start.3 = ((bf16[64,1,20,128]{3,2,1,0:T(8,128)(2,1)}), bf16[64,1,20,128]{3,2,1,0:T(8,128)(2,1)}, u32[]{:S(2)}, u32[]{:S(2)}) async-start(bf16[64,1,20,128]{3,2,1,0:T(8,128)(2,1)} %broadcast_in_dim.23), calls=%async_computation.3 | async-start | bytes 786432 | tf_op jit(solution)/shard_map/all_to_all | solution.py:30
  120.0 5.4 %copy-start.4 = (f32[1024]{0:T(1024)S(1)}, f32[1024]{0:T(1024)}, u32[]{:S(2)}) copy-start(f32[1024]{0:T(1024)} %param.10) | copy-start | bytes 12292
  145.7 13.6 %copy-start.2 = (f32[16,1024]{1,0:T(8,128)S(1)}, f32[16,1024]{1,0:T(8,128)}, u32[]{:S(2)}) copy-start(f32[16,1024]{1,0:T(8,128)} %broadcast_add_fusion) | copy-start | bytes 196612
where the time goes:
time: 166 us
  local copies, waits for them, and re-layouts  57.6 us (35%)
  blocking collectives  48.8 us (29%)
  waiting for transfers between devices  23.4 us (14%)
  matrix products  20.7 us (12%)
  starting transfers between devices  12.9 us (8%)
    all_to_all x1, blocking collectives, summed_on_arrival(): tiles = lax.all_to_all(split_up(shard, dim, size), axis, 0, 0, tiled=True)  32 us
    all_to_all x2, waiting for transfers between devices, copy_for_each(): lax.all_to_all(jnp.broadcast_to(shard[None], (size, *shard.shape)), axis,...  23.4 us
    all_to_all x1, blocking collectives, copy_for_each(): lax.all_to_all(jnp.broadcast_to(shard[None], (size, *shard.shape)), axis,...  16.9 us
    convert_element_type x1, local copies, waits for them, and re-layouts, shards(): upper = jnp.einsum('bia,bpis->pabs', left_all, square, preferred_element_...  13.6 us
    all_to_all x2, starting transfers between devices, copy_for_each(): lax.all_to_all(jnp.broadcast_to(shard[None], (size, *shard.shape)), axis,...  12.9 us
    gather x1, local copies, waits for them, and re-layouts, shards(): right = half[:, :, highs[:, None] + col_span[None, :]]  11.1 us
    convert_element_type x1, local copies, waits for them, and re-layouts, shards(): half = jnp.einsum('pab,nb->pan', amplitudes, virtuals, preferred_element_...  7.94 us
    dot_general x1, matrix products, shards(): jnp.einsum('pabs,bsn->pan', upper, right_rows, preferred_element_type=jnp...  6.18 us
  transfers between devices with their start and end apart: 2, of which 2 were waited for; matrix products, arithmetic and copies ran while one was open for 4% of the time, Pallas kernels for 0%

commit v1 on v0

v1 whole, which is shorter than its diff:
```python
import functools

import jax
import jax.numpy as jnp
from jax import lax
from jax.experimental import pallas as pl
from jax.experimental.pallas import tpu as pltpu
from jax.sharding import PartitionSpec as P

ROW = 8
COL = 16
WIDTH = ROW * COL
LANES = 128
GROUP = LANES // COL
BF = jnp.bfloat16
F32 = jnp.float32
MESH = pl.DeviceIdType.MESH
PAD = 24
VMEM_LIMIT = 60 * 1024 * 1024


def permutation(size):
    row = lax.broadcasted_iota(jnp.int32, (size, size), 0)
    col = lax.broadcasted_iota(jnp.int32, (size, size), 1)
    target = ((row // COL) % GROUP) * LANES + (row // LANES) * COL + row % COL
    return jnp.where(col == target, 1.0, 0.0).astype(BF)


def project_kernel(off, amp, virt, part, right, spread_e, vf, half, lrows, lt, spread_a, cells, stacked):
    nao, next_ = virt.shape
    rows = amp.shape[0]
    pairs = rows // COL
    nblk = off.shape[1]
    groups = nblk // GROUP
    me = lax.axis_index("sp")
    tile0 = me * COL // LANES
    sub0 = pl.multiple_of((me * COL) % LANES, COL)

    chunk = 128
    whole = nao // chunk

    def widen(c, _):
        at = pl.multiple_of(c * chunk, chunk)
        for t in range(next_ // LANES):
            vf[t, pl.ds(at, chunk), :] = virt[pl.ds(at, chunk), t * LANES : (t + 1) * LANES].astype(F32)
        return 0

    lax.fori_loop(0, whole, widen, 0)
    if nao % chunk:
        for t in range(next_ // LANES):
            vf[t, whole * chunk : nao, :] = virt[whole * chunk : nao, t * LANES : (t + 1) * LANES].astype(F32)

    def pick(b, _):
        to = pl.multiple_of(b * COL, COL)
        for t in range(next_ // LANES):
            right[pl.ds(to, COL), t * LANES : (t + 1) * LANES] = vf[t, pl.ds(off[1, b], COL), :].astype(BF)
        lrows[pl.ds(pl.multiple_of(b * ROW, ROW), ROW), :] = vf[tile0, pl.ds(off[0, b], ROW), :]
        return 0

    lax.fori_loop(0, nblk, pick, 0)

    owner = lax.broadcasted_iota(jnp.int32, (nblk, nblk * COL), 1) // COL
    repeat = jnp.where(lax.broadcasted_iota(jnp.int32, (nblk, nblk * COL), 0) == owner, 1.0, 0.0).astype(BF)
    for i in range(ROW):
        lt[...] = lrows[pl.ds(i, nblk, stride=ROW), :].T
        mine = jnp.dot(lt[pl.ds(sub0, COL), :].astype(BF), repeat, preferred_element_type=F32)
        spread_e[i * COL : (i + 1) * COL, :] = mine
        for g in range(groups):
            spread_a[g, pl.ds(i, COL, stride=ROW), :] = mine[:, g * LANES : (g + 1) * LANES]

    step = 256
    for n in range(0, nblk * COL, step):
        got = lax.dot_general(
            amp[...], right[n : n + step, :], (((1,), (1,)), ((), ())), preferred_element_type=F32
        )
        got = got.astype(BF).astype(F32)
        for t in range(step // LANES):
            half[n // LANES + t] = got[:, t * LANES : (t + 1) * LANES]

    cells[...] = jnp.zeros_like(cells)
    for g in range(groups):

        def contract(p, _):
            total = jnp.zeros((ROW, LANES), F32)
            for a in range(COL):
                line = half[g, pl.ds(p * COL + a, ROW, stride=0), :]
                total = total + spread_a[g, a * ROW : (a + 1) * ROW, :] * line
            cells[pl.ds(pl.multiple_of(g * PAD * ROW + p * ROW, ROW), ROW), :] = total
            return 0

        lax.fori_loop(0, pairs, contract, 0, unroll=2)
        for i in range(ROW):
            stacked[g * PAD : (g + 1) * PAD, i * LANES : (i + 1) * LANES] = cells[
                pl.ds(g * PAD * ROW + i, PAD, stride=ROW), :
            ]
    moved = jnp.dot(stacked[...].astype(BF), permutation(GROUP * LANES), preferred_element_type=F32)
    for g in range(groups):
        for v in range(GROUP):
            part[v % 2, (g * GROUP + v) // 2] = moved[
                g * PAD : g * PAD + pairs, v * LANES : (v + 1) * LANES
            ].astype(BF)


def project(offsets, amp, virtuals, pairs):
    nao, next_ = virtuals.shape
    nblk = offsets.shape[1]
    rows = amp.shape[0]
    groups = nblk // GROUP
    vmem = pl.BlockSpec(memory_space=pltpu.VMEM)
    return pl.pallas_call(
        project_kernel,
        out_shape=(
            jax.ShapeDtypeStruct((2, nblk // 2, pairs, WIDTH), BF),
            jax.ShapeDtypeStruct((nblk * COL, next_), BF),
            jax.ShapeDtypeStruct((ROW * COL, nblk * COL), F32),
        ),
        in_specs=[pl.BlockSpec(memory_space=pltpu.SMEM), vmem, vmem],
        out_specs=(vmem, vmem, vmem),
        scratch_shapes=[
            pltpu.VMEM((next_ // LANES, nao, LANES), F32),
            pltpu.VMEM((groups, rows, LANES), F32),
            pltpu.VMEM((nblk * ROW, LANES), F32),
            pltpu.VMEM((LANES, nblk), F32),
            pltpu.VMEM((groups, COL * ROW, LANES), F32),
            pltpu.VMEM((groups * PAD * ROW, LANES), F32),
            pltpu.VMEM((groups * PAD, ROW * LANES), F32),
        ],
        compiler_params=pltpu.CompilerParams(vmem_limit_bytes=VMEM_LIMIT),
        name="project",
    )(offsets, amp, virtuals)


def far_first(t, size):
    return size // 2 + (1 - 2 * (t % 2)) * ((t + 1) // 2)


def exchange_kernel(
    nx, ny,
    screened, counts, part, integrals, coupling, mixed_all,
    pairsum, outgoing, arrived, ao_own, ao_all, chosen, raw_own, raw_all, raw_rows, mix_own,
    pair_s, pair_r, rs_s, rs_r, ag_s, ag_r, fw_s, fw_r, z_s, z_r, mg_s, mg_r, mf_s, mf_r,
):
    sp = lax.axis_index("sp")
    z = lax.axis_index("pb")
    nz = lax.axis_size("pb")
    core = sp % 2
    chip = sp // 2
    x = chip % nx
    y = chip // nx
    chips = nx * ny
    other = (chip * 2 + (1 - core), z)
    pairs = ao_own.shape[0]

    def peer(t):
        dy = far_first(t // nx, ny)
        dx = far_first(t % nx, nx)
        return ((y + dy) % ny) * nx + (x + dx) % nx

    def source(t):
        dy = far_first(t // nx, ny)
        dx = far_first(t % nx, nx)
        return ((y + ny - dy) % ny) * nx + (x + nx - dx) % nx

    barrier = pltpu.get_barrier_semaphore()
    pl.semaphore_signal(barrier, inc=1, device_id=other, device_id_type=MESH)

    def greet(t, _):
        pl.semaphore_signal(barrier, inc=1, device_id=(peer(t) * 2 + core, z), device_id_type=MESH)
        return 0

    lax.fori_loop(0, chips - 1, greet, 0)

    def greet_z(t, _):
        pl.semaphore_signal(barrier, inc=1, device_id=(sp, (z + 1 + t) % nz), device_id_type=MESH)
        return 0

    lax.fori_loop(0, nz - 1, greet_z, 0)
    pl.semaphore_wait(barrier, chips + nz - 1)

    swap = pltpu.make_async_remote_copy(
        part.at[1 - core], pairsum, pair_s, pair_r, device_id=other, device_id_type=MESH
    )
    swap.start()
    swap.wait_recv()
    outgoing[...] = (part[core].astype(F32) + pairsum[...].astype(F32)).astype(BF)

    def scatter(t):
        to = peer(t)
        return pltpu.make_async_remote_copy(
            outgoing.at[to], arrived.at[chip], rs_s.at[t], rs_r.at[t],
            device_id=(to * 2 + core, z), device_id_type=MESH,
        )

    def scatter_wait(t, total):
        come = source(t)
        pltpu.make_async_remote_copy(
            outgoing.at[come], arrived.at[come], rs_s.at[t], rs_r.at[t],
            device_id=(come * 2 + core, z), device_id_type=MESH,
        ).wait_recv()
        return total + arrived[come].astype(F32)

    def go(t, _):
        scatter(t).start()
        return 0

    lax.fori_loop(0, chips - 1, go, 0)
    total = lax.fori_loop(0, chips - 1, lambda t, c: scatter_wait(chips - 2 - t, c), outgoing[chip].astype(F32))
    ao_own[...] = total.astype(BF)

    def gather(own, landing, send, recv, fsend, frecv):
        def to_peer(t):
            return pltpu.make_async_remote_copy(
                own, landing.at[core, chip], send.at[t], recv.at[t],
                device_id=(peer(t) * 2 + core, z), device_id_type=MESH,
            )

        def from_peer(t):
            come = source(t)
            return pltpu.make_async_remote_copy(
                own, landing.at[core, come], send.at[t], recv.at[t],
                device_id=(come * 2 + core, z), device_id_type=MESH,
            )

        def forward(t):
            come = source(t)
            return pltpu.make_async_remote_copy(
                landing.at[core, come], landing.at[core, come], fsend.at[t], frecv.at[t],
                device_id=other, device_id_type=MESH,
            )

        def from_other(t):
            come = source(t)
            return pltpu.make_async_remote_copy(
                landing.at[1 - core, come], landing.at[1 - core, come], fsend.at[t], frecv.at[t],
                device_id=other, device_id_type=MESH,
            )

        def begin(t, _):
            to_peer(t).start()
            return 0

        lax.fori_loop(0, chips - 1, begin, 0)
        mine = pltpu.make_async_remote_copy(
            own, landing.at[core, chip], fsend.at[chips - 1], frecv.at[chips - 1],
            device_id=other, device_id_type=MESH,
        )
        mine.start()
        landing[core, chip] = own[...]

        def relay(t, _):
            u = chips - 2 - t
            from_peer(u).wait_recv()
            forward(u).start()
            return 0

        lax.fori_loop(0, chips - 1, relay, 0)
        pltpu.make_async_remote_copy(
            own, landing.at[1 - core, chip], fsend.at[chips - 1], frecv.at[chips - 1],
            device_id=other, device_id_type=MESH,
        ).wait_recv()

        def settle(t, _):
            from_other(chips - 2 - t).wait_recv()
            return 0

        lax.fori_loop(0, chips - 1, settle, 0)

        def drain():
            def one(t, _):
                to_peer(t).wait_send()
                forward(t).wait_send()
                return 0

            lax.fori_loop(0, chips - 1, one, 0)
            mine.wait_send()

        return drain

    drain_ao = gather(ao_own, ao_all, ag_s, ag_r, fw_s, fw_r)

    slots = screened.shape[1]
    for k in range(slots):
        b = screened[0, k]
        tile = ao_all[b % 2, b // 2].astype(F32)
        chosen[:, k * WIDTH : (k + 1) * WIDTH] = jnp.where(k < counts[0], tile, 0.0).astype(BF)
    raw = lax.dot_general(
        chosen[...], integrals[...], (((1,), (1,)), ((), ())), preferred_element_type=F32
    )
    raw_own[...] = raw.astype(BF)

    def along(t):
        return pltpu.make_async_remote_copy(
            raw_own, raw_all.at[z], z_s.at[t], z_r.at[t],
            device_id=(sp, (z + far_first(t, nz)) % nz), device_id_type=MESH,
        )

    def along_in(t):
        come = (z + nz - far_first(t, nz)) % nz
        return pltpu.make_async_remote_copy(
            raw_own, raw_all.at[come], z_s.at[t], z_r.at[t],
            device_id=(sp, come), device_id_type=MESH,
        )

    for t in range(nz - 1):
        along(t).start()
    raw_all[z] = raw_own[...]
    for t in range(nz - 1):
        along_in(t).wait_recv()
    for q in range(nz):
        raw_rows[q * pairs : (q + 1) * pairs, :] = raw_all[q].astype(F32)
    mix = jnp.dot(coupling[...], raw_rows[...].astype(BF), preferred_element_type=F32)
    mix_own[...] = mix.astype(BF)

    drain_mix = gather(mix_own, mixed_all, mg_s, mg_r, mf_s, mf_r)

    swap.wait_send()

    def drain_rs(t, _):
        scatter(t).wait_send()
        return 0

    lax.fori_loop(0, chips - 1, drain_rs, 0)
    drain_ao()
    for t in range(nz - 1):
        along(t).wait_send()
    drain_mix()


def exchange(screened, counts, part, integrals, coupling, nx, ny, nz):
    _, chips, pairs, width = part.shape
    slots = screened.shape[1]
    vmem = pl.BlockSpec(memory_space=pltpu.VMEM)
    smem = pl.BlockSpec(memory_space=pltpu.SMEM)
    dma = pltpu.SemaphoreType.DMA
    return pl.pallas_call(
        functools.partial(exchange_kernel, nx, ny),
        out_shape=jax.ShapeDtypeStruct(part.shape, BF),
        in_specs=[smem, smem, vmem, vmem, vmem],
        out_specs=vmem,
        scratch_shapes=[
            pltpu.VMEM((chips, pairs, width), BF),
            pltpu.VMEM((chips, pairs, width), BF),
            pltpu.VMEM((chips, pairs, width), BF),
            pltpu.VMEM((pairs, width), BF),
            pltpu.VMEM((2, chips, pairs, width), BF),
            pltpu.VMEM((pairs, slots * width), BF),
            pltpu.VMEM((pairs, width), BF),
            pltpu.VMEM((nz, pairs, width), BF),
            pltpu.VMEM((nz * pairs, width), F32),
            pltpu.VMEM((pairs, width), BF),
            dma, dma,
            dma((chips,)), dma((chips,)),
            dma((chips,)), dma((chips,)), dma((chips,)), dma((chips,)),
            dma((nz,)), dma((nz,)),
            dma((chips,)), dma((chips,)), dma((chips,)), dma((chips,)),
        ],
        compiler_params=pltpu.CompilerParams(
            collective_id=0, has_side_effects=True, vmem_limit_bytes=VMEM_LIMIT
        ),
        name="exchange",
    )(screened, counts, part, integrals, coupling)


def finish_kernel(mixed_all, right, spread_e, amp, energies, out, blocks, cells, upper):
    _, chips, pairs, _ = mixed_all.shape
    rows, next_ = amp.shape
    groups = chips * 2 // GROUP
    me = lax.axis_index("sp")
    blocks[...] = jnp.zeros_like(blocks)
    for g in range(groups):
        for v in range(GROUP):
            blocks[g * PAD : g * PAD + pairs, v * LANES : (v + 1) * LANES] = mixed_all[
                v % 2, (g * GROUP + v) // 2
            ].astype(F32)
    moved = jnp.dot(blocks[...].astype(BF), permutation(GROUP * LANES), preferred_element_type=F32)
    for i in range(ROW):
        cells[i] = moved[:, i * LANES : (i + 1) * LANES]
    for g in range(groups):
        lanes = slice(g * LANES, (g + 1) * LANES)

        def lift(p, _):
            total = jnp.zeros((COL, LANES), F32)
            for i in range(ROW):
                line = cells[i, pl.ds(g * PAD + p, ROW, stride=0), :]
                line = jnp.concatenate([line, line], axis=0)
                total = total + spread_e[i * COL : (i + 1) * COL, lanes] * line
            upper[pl.ds(pl.multiple_of(p * COL, COL), COL), lanes] = total.astype(BF)
            return 0

        lax.fori_loop(0, pairs, lift, 0, unroll=2)
    hit = lax.broadcasted_iota(jnp.int32, (COL, next_), 1) == (
        lax.broadcasted_iota(jnp.int32, (COL, next_), 0) + me * COL
    )
    own = jnp.sum(jnp.where(hit, energies[...], 0.0), axis=1, keepdims=True)
    step = 256
    for n in range(0, next_, step):
        inner = jnp.dot(upper[...], right[:, n : n + step], preferred_element_type=F32)
        diag = own + energies[:, n : n + step]
        term = amp[:, n : n + step].astype(F32).reshape(pairs, COL, step) * diag[None]
        out[:, n : n + step] = (inner + term.reshape(rows, step)).astype(BF)


def finish(mixed_all, right, spread_e, amp, energies):
    _, chips, pairs, _ = mixed_all.shape
    groups = chips * 2 // GROUP
    vmem = pl.BlockSpec(memory_space=pltpu.VMEM)
    return pl.pallas_call(
        finish_kernel,
        out_shape=jax.ShapeDtypeStruct(amp.shape, BF),
        in_specs=[vmem] * 5,
        out_specs=vmem,
        scratch_shapes=[
            pltpu.VMEM((groups * PAD, GROUP * LANES), F32),
            pltpu.VMEM((ROW, groups * PAD, LANES), F32),
            pltpu.VMEM((amp.shape[0], groups * LANES), BF),
        ],
        compiler_params=pltpu.CompilerParams(vmem_limit_bytes=VMEM_LIMIT),
        name="finish",
    )(mixed_all, right, spread_e, amp, energies)


NX, NY, NZ = 4, 8, 8


def shards(amplitudes, virtuals, energies, integrals, screened, counts, offsets, coupling):
    pairs, ext, next_ = amplitudes.shape
    amp = amplitudes.reshape(pairs * ext, next_)
    part, right, spread_e = project(offsets, amp, virtuals, pairs)
    mixed_all = exchange(screened, counts, part, integrals, coupling, NX, NY, NZ)
    out = finish(mixed_all, right, spread_e, amp, energies.reshape(1, next_))
    return out.reshape(pairs, ext, next_)


def solution(mesh):
    return jax.shard_map(
        shards,
        mesh=mesh,
        in_specs=(
            P("pb", "sp", None),
            P(),
            P(),
            P("sp", None),
            P("sp", None),
            P("sp"),
            P(),
            P("pb", None),
        ),
        out_specs=P("pb", "sp", None),
        check_vma=False,
    )
```

time: 166 us -> 69.2 us (0.42)
  Pallas kernels: 0 us -> 68.4 us
  local copies, waits for them, and re-layouts: 57.6 us -> 0 us
  blocking collectives: 48.8 us -> 0 us
  waiting for transfers between devices: 23.4 us -> 0 us
  matrix products: 20.7 us -> 0 us
  starting transfers between devices: 12.9 us -> 0 us
    pallas_call x0 -> x3, Pallas kernels: none -> 68.4 us  [the longest x1 54.6 us: exchange(): pl.pallas_call(functools.partial(exchange_kernel, nx, ny), out_shape=jax....]
    all_to_all x2 -> x0, blocking collectives: 48.8 us -> none  [the longest x1 32 us: summed_on_arrival(): tiles = lax.all_to_all(split_up(shard, dim, size), axis, 0, 0, tiled=True)]
    all_to_all x2 -> x0, waiting for transfers between devices: 23.4 us -> none  [copy_for_each(): lax.all_to_all(jnp.broadcast_to(shard[None], (size, *shard.shape)), axis,...]
    convert_element_type x2 -> x0, local copies, waits for them, and re-layouts: 21.6 us -> none  [the longest x1 13.6 us: shards(): upper = jnp.einsum('bia,bpis->pabs', left_all, square, preferred_element_...]
    dot_general x6 -> x0, matrix products: 20.7 us -> none  [the longest x1 6.18 us: shards(): jnp.einsum('pabs,bsn->pan', upper, right_rows, preferred_element_type=jnp...]
    gather x4 -> x0, local copies, waits for them, and re-layouts: 18.3 us -> none  [the longest x1 11.1 us: shards(): right = half[:, :, highs[:, None] + col_span[None, :]]]
    all_to_all x2 -> x0, starting transfers between devices: 12.9 us -> none  [copy_for_each(): lax.all_to_all(jnp.broadcast_to(shard[None], (size, *shard.shape)), axis,...]
    another operation x3 -> x0, local copies, waits for them, and re-layouts: 7.54 us -> none  [the longest x1 4.36 us: shards(): square = k_all.reshape(nblk, pairs, SHELL_ROW, SHELL_COL)]
  transfers between devices with their start and end apart: 2 -> 0, of which waited for: 2 -> 0; matrix products, arithmetic and copies ran while one was open for 4% -> 0% of each run, Pallas kernels for 0% -> 0%
where the time goes in v1:
time: 69.2 us; the launch traced here: 69 us
  Pallas kernels  68.4 us (99%)
    pallas_call x1, Pallas kernels, exchange(): pl.pallas_call(functools.partial(exchange_kernel, nx, ny), out_shape=jax....  54.6 us
    pallas_call x1, Pallas kernels, project(): pl.pallas_call(project_kernel, out_shape=(jax.ShapeDtypeStruct((2, nblk /...  7.96 us
    pallas_call x1, Pallas kernels, finish(): pl.pallas_call(finish_kernel, out_shape=jax.ShapeDtypeStruct(amp.shape, B...  5.75 us

profile of v1, /device:TPU:1, one launch (start us, length us, event | category | flops | bytes accessed | tf_op | source)
XLA Modules:
  0.0 69.0 jit_solution(11735944829080872175)
XLA Ops:
  0.7 8.0 %project.1 = (bf16[2,32,20,128]{3,2,1,0:T(8,128)(2,1)}, bf16[1024,1024]{1,0:T(8,128)(2,1)}, f32[128,1024]{1,0:T(8,128)}) custom-call(s32[2,64]{1,0:T(2,128)} %off.1, bf16[320,1024]{1,0:T(8,128)(2,1)} %bitcast.3, bf16[1400,1024]{1,0:T(8,128)(2,1)} %virt.1), custom_call_target="tpu_custom_call" | custom-call | tf_op jit(solution)/shard_map/project/pallas_call | solution.py:110
  8.6 54.6 %exchange.1.mixed_all = bf16[2,32,20,128]{3,2,1,0:T(8,128)(2,1)} custom-call(s32[1,16]{1,0:T(1,128)} %screened.1, s32[1]{0:T(128)S(6)} %copy.9.counts, bf16[2,32,20,128]{3,2,1,0:T(8,128)(2,1)} %get-tuple-element.8.part, bf16[128,2048]{1,0:T(8,128)(2,1)} %integrals.1, bf16[20,160]{1,0:T(8,128)(2,1)} %coupling.1), custom_call_target="tpu_custom_call" | custom-call | tf_op jit(solution)/shard_map/exchange/pallas_call | solution.py:335
  63.3 5.8 %finish.1 = bf16[320,1024]{1,0:T(8,128)(2,1)} custom-call(bf16[2,32,20,128]{3,2,1,0:T(8,128)(2,1)} %exchange.1.mixed_all, bf16[1024,1024]{1,0:T(8,128)(2,1)} %get-tuple-element.9.right, f32[128,1024]{1,0:T(8,128)} %get-tuple-element.10.spread_e, bf16[320,1024]{1,0:T(8,128)(2,1)} %bitcast.4, f32[1,1024]{1,0:T(1,128)} %bitcast.5), custom_call_target="tpu_custom_call" | custom-call | tf_op jit(solution)/shard_map/finish/pallas_call | solution.py:407

commit v2 on v1

v2 whole, which is shorter than its diff:
```python
import functools

import jax
import jax.numpy as jnp
from jax import lax
from jax.experimental import pallas as pl
from jax.experimental.pallas import tpu as pltpu
from jax.sharding import PartitionSpec as P

ROW = 8
COL = 16
WIDTH = ROW * COL
LANES = 128
GROUP = LANES // COL
SUB = 4
BF = jnp.bfloat16
F32 = jnp.float32
MESH = pl.DeviceIdType.MESH
PAD = 24
VROWS = 176
NX, NY = 4, 8


def far_first(t, size):
    return size // 2 + (1 - 2 * (t % 2)) * ((t + 1) // 2)


def residual_kernel(
    off, screened, counts, virt, amp_hbm, integrals_hbm, coupling, energies, out,
    right, upper, diag, vbuf, vf, amp, integrals, perm, half, lrows, lt, spread_e, spread_a, cells, stacked,
    part, pairsum, outgoing, arrived, ao_own, ao_all, chosen, raw_own, raw_all, raw_rows, mix_own, mixed_all,
    local_s, pair_s, pair_r, rs_s, rs_r, ag_s, ag_r, fw_s, fw_r, z_s, z_r, mg_s, mg_r, mf_s, mf_r,
):
    nao, next_ = virt.shape
    rows = amp.shape[0]
    pairs = rows // COL
    pieces = pairs // SUB
    nblk = off.shape[1]
    groups = nblk // GROUP
    tiles = next_ // LANES
    slots = screened.shape[1]
    chips = NX * NY

    sp = lax.axis_index("sp")
    z = lax.axis_index("pb")
    nz = lax.axis_size("pb")
    core = sp % 2
    chip = sp // 2
    x = chip % NX
    y = chip // NX
    other = (chip * 2 + (1 - core), z)

    def peer(t):
        dy = far_first(t // NX, NY)
        dx = far_first(t % NX, NX)
        return ((y + dy) % NY) * NX + (x + dx) % NX

    def source(t):
        dy = far_first(t // NX, NY)
        dx = far_first(t % NX, NX)
        return ((y + NY - dy) % NY) * NX + (x + NX - dx) % NX

    barrier = pltpu.get_barrier_semaphore()

    def greet(t, _):
        pl.semaphore_signal(barrier, inc=1, device_id=(peer(t) * 2 + core, z), device_id_type=MESH)
        return 0

    lax.fori_loop(0, chips - 1, greet, 0)

    def greet_z(t, _):
        pl.semaphore_signal(barrier, inc=1, device_id=(sp, (z + 1 + t) % nz), device_id_type=MESH)
        return 0

    lax.fori_loop(0, nz - 1, greet_z, 0)
    pl.semaphore_signal(barrier, inc=1, device_id=other, device_id_type=MESH)

    starts = list(range(0, nao, VROWS))
    loads = []
    for c, at in enumerate(starts):
        size = min(VROWS, nao - at)
        loads.append(
            pltpu.make_async_copy(virt.at[pl.ds(at, size)], vbuf.at[pl.ds(at, size)], local_s.at[c])
        )
    amp_load = pltpu.make_async_copy(amp_hbm, amp, local_s.at[len(starts)])
    int_load = pltpu.make_async_copy(integrals_hbm, integrals, local_s.at[len(starts) + 1])
    for load in loads:
        load.start()
    amp_load.start()
    int_load.start()

    def mark(u, _):
        shape = (LANES, GROUP * LANES)
        row = lax.broadcasted_iota(jnp.int32, shape, 0)
        col = lax.broadcasted_iota(jnp.int32, shape, 1)
        target = (row // COL) * LANES + u * COL + row % COL
        perm[pl.ds(pl.multiple_of(u * LANES, LANES), LANES), :] = jnp.where(col == target, 1.0, 0.0).astype(BF)
        return 0

    lax.fori_loop(0, GROUP, mark, 0)
    cells[...] = jnp.zeros_like(cells)

    for c, at in enumerate(starts):
        size = min(VROWS, nao - at)
        loads[c].wait()
        for t in range(tiles):
            vf[t, at : at + size, :] = vbuf[at : at + size, t * LANES : (t + 1) * LANES].astype(F32)

    tile0 = sp * COL // LANES
    sub0 = pl.multiple_of((sp * COL) % LANES, COL)

    def pick(b, _):
        to = pl.multiple_of(b * COL, COL)
        for t in range(tiles):
            right[pl.ds(to, COL), t * LANES : (t + 1) * LANES] = vf[t, pl.ds(off[1, b], COL), :].astype(BF)
        lrows[pl.ds(pl.multiple_of(b * ROW, ROW), ROW), :] = vf[tile0, pl.ds(off[0, b], ROW), :]
        return 0

    lax.fori_loop(0, nblk, pick, 0, unroll=2)

    owner = lax.broadcasted_iota(jnp.int32, (nblk, nblk * COL), 1) // COL
    repeat = jnp.where(lax.broadcasted_iota(jnp.int32, (nblk, nblk * COL), 0) == owner, 1.0, 0.0).astype(BF)
    for i in range(ROW):
        lt[i] = lrows[pl.ds(i, nblk, stride=ROW), :].T
        mine = jnp.dot(lt[i, pl.ds(sub0, COL), :].astype(BF), repeat, preferred_element_type=F32)
        spread_e[i * COL : (i + 1) * COL, :] = mine
        for g in range(groups):
            spread_a[g, pl.ds(i, COL, stride=ROW), :] = mine[:, g * LANES : (g + 1) * LANES]

    amp_load.wait()
    step = 256
    for n in range(0, nblk * COL, step):
        got = lax.dot_general(
            amp[...], right[n : n + step, :], (((1,), (1,)), ((), ())), preferred_element_type=F32
        )
        got = got.astype(BF).astype(F32)
        for t in range(step // LANES):
            half[n // LANES + t] = got[:, t * LANES : (t + 1) * LANES]

    for g in range(groups):

        def contract(p, _):
            total = jnp.zeros((ROW, LANES), F32)
            for a in range(COL):
                line = half[g, pl.ds(p * COL + a, ROW, stride=0), :]
                total = total + spread_a[g, a * ROW : (a + 1) * ROW, :] * line
            cells[pl.ds(pl.multiple_of(g * PAD * ROW + p * ROW, ROW), ROW), :] = total
            return 0

        lax.fori_loop(0, pairs, contract, 0, unroll=2)
        for i in range(ROW):
            stacked[g * PAD : (g + 1) * PAD, i * LANES : (i + 1) * LANES] = cells[
                pl.ds(g * PAD * ROW + i, PAD, stride=ROW), :
            ].astype(BF)
    moved = jnp.dot(stacked[...], perm[...], preferred_element_type=F32)
    for g in range(groups):
        for v in range(GROUP):
            for j in range(pieces):
                part[v % 2, (g * GROUP + v) // 2, j] = moved[
                    g * PAD + j * SUB : g * PAD + (j + 1) * SUB, v * LANES : (v + 1) * LANES
                ].astype(BF)

    hit = lax.broadcasted_iota(jnp.int32, (COL, next_), 1) == (
        lax.broadcasted_iota(jnp.int32, (COL, next_), 0) + sp * COL
    )
    own_energy = jnp.sum(jnp.where(hit, energies[...], 0.0), axis=1, keepdims=True)

    pl.semaphore_wait(barrier, chips + nz - 1)

    def swap(t):
        to = peer(t)
        return pltpu.make_async_remote_copy(
            part.at[1 - core, to], pairsum.at[to], pair_s.at[t], pair_r.at[t],
            device_id=other, device_id_type=MESH,
        )

    def scatter(t):
        to = peer(t)
        return pltpu.make_async_remote_copy(
            outgoing.at[to], arrived.at[chip], rs_s.at[t], rs_r.at[t],
            device_id=(to * 2 + core, z), device_id_type=MESH,
        )

    def swap_go(t, _):
        swap(t).start()
        return 0

    def pair_total(t):
        to = peer(t)
        swap(t).wait_recv()
        return part[core, to].astype(F32) + pairsum[to].astype(F32)

    def scatter_go(t, _):
        outgoing[peer(t)] = pair_total(t).astype(BF)
        scatter(t).start()
        return 0

    def scatter_in(t, total):
        u = chips - 2 - t
        come = source(u)
        pltpu.make_async_remote_copy(
            outgoing.at[come], arrived.at[come], rs_s.at[u], rs_r.at[u],
            device_id=(come * 2 + core, z), device_id_type=MESH,
        ).wait_recv()
        return total + arrived[come].astype(F32)

    lax.fori_loop(0, chips, swap_go, 0)
    lax.fori_loop(0, chips - 1, scatter_go, 0)

    def diagonal(p, _):
        at = pl.multiple_of(p * COL, COL)
        diag[pl.ds(at, COL), :] = (own_energy + energies[...]) * amp[pl.ds(at, COL), :].astype(F32)
        return 0

    lax.fori_loop(0, pairs, diagonal, 0)
    total = lax.fori_loop(0, chips - 1, scatter_in, pair_total(chips - 1))
    ao_own[...] = total.astype(BF)

    def gather(own, landing, send, recv, fsend, frecv):
        def to_peer(t):
            return pltpu.make_async_remote_copy(
                own, landing.at[core, chip], send.at[t], recv.at[t],
                device_id=(peer(t) * 2 + core, z), device_id_type=MESH,
            )

        def from_peer(t):
            come = source(t)
            return pltpu.make_async_remote_copy(
                own, landing.at[core, come], send.at[t], recv.at[t],
                device_id=(come * 2 + core, z), device_id_type=MESH,
            )

        def forward(t):
            come = source(t)
            return pltpu.make_async_remote_copy(
                landing.at[core, come], landing.at[core, come], fsend.at[t], frecv.at[t],
                device_id=other, device_id_type=MESH,
            )

        def from_other(t):
            come = source(t)
            return pltpu.make_async_remote_copy(
                landing.at[1 - core, come], landing.at[1 - core, come], fsend.at[t], frecv.at[t],
                device_id=other, device_id_type=MESH,
            )

        def begin(t, _):
            to_peer(t).start()
            return 0

        lax.fori_loop(0, chips - 1, begin, 0)
        mine = pltpu.make_async_remote_copy(
            own, landing.at[core, chip], fsend.at[chips - 1], frecv.at[chips - 1],
            device_id=other, device_id_type=MESH,
        )
        mine.start()
        landing[core, chip] = own[...]

        def relay(t, _):
            u = chips - 2 - t
            from_peer(u).wait_recv()
            forward(u).start()
            return 0

        lax.fori_loop(0, chips - 1, relay, 0)
        pltpu.make_async_remote_copy(
            own, landing.at[1 - core, chip], fsend.at[chips - 1], frecv.at[chips - 1],
            device_id=other, device_id_type=MESH,
        ).wait_recv()

        def settle(t, _):
            from_other(chips - 2 - t).wait_recv()
            return 0

        lax.fori_loop(0, chips - 1, settle, 0)

        def drain():
            def one(t, _):
                to_peer(t).wait_send()
                forward(t).wait_send()
                return 0

            lax.fori_loop(0, chips - 1, one, 0)
            mine.wait_send()

        return drain

    drain_ao = gather(ao_own, ao_all, ag_s, ag_r, fw_s, fw_r)

    for k in range(slots):
        b = screened[0, k]
        tile = jnp.where(k < counts[0], ao_all[b % 2, b // 2].astype(F32), 0.0)
        for j in range(pieces):
            chosen[j * SUB : (j + 1) * SUB, k * WIDTH : (k + 1) * WIDTH] = tile[j]
    int_load.wait()
    raw = lax.dot_general(
        chosen[...].astype(BF), integrals[...], (((1,), (1,)), ((), ())), preferred_element_type=F32
    )
    for j in range(pieces):
        raw_own[j] = raw[j * SUB : (j + 1) * SUB, :].astype(BF)

    def along(t):
        return pltpu.make_async_remote_copy(
            raw_own, raw_all.at[z], z_s.at[t], z_r.at[t],
            device_id=(sp, (z + far_first(t, nz)) % nz), device_id_type=MESH,
        )

    def along_in(t):
        come = (z + nz - far_first(t, nz)) % nz
        return pltpu.make_async_remote_copy(
            raw_own, raw_all.at[come], z_s.at[t], z_r.at[t],
            device_id=(sp, come), device_id_type=MESH,
        )

    for t in range(nz - 1):
        along(t).start()
    raw_all[z] = raw_own[...]
    for t in range(nz - 1):
        along_in(t).wait_recv()
    for q in range(nz):
        for j in range(pieces):
            at = q * pairs + j * SUB
            raw_rows[at : at + SUB, :] = raw_all[q, j].astype(F32)
    mix = jnp.dot(coupling[...], raw_rows[...].astype(BF), preferred_element_type=F32)
    for j in range(pieces):
        mix_own[j] = mix[j * SUB : (j + 1) * SUB, :].astype(BF)

    drain_mix = gather(mix_own, mixed_all, mg_s, mg_r, mf_s, mf_r)

    for b in range(nblk):
        block = mixed_all[b % 2, b // 2].astype(F32)
        for j in range(pieces):
            cells[b * PAD + j * SUB : b * PAD + (j + 1) * SUB, :] = block[j]
    for g in range(groups):
        for v in range(GROUP):
            at = (g * GROUP + v) * PAD
            stacked[g * PAD : (g + 1) * PAD, v * LANES : (v + 1) * LANES] = cells[at : at + PAD, :].astype(BF)
    moved = jnp.dot(stacked[...], perm[...], preferred_element_type=F32)
    for i in range(ROW):
        cells[i * groups * PAD : (i + 1) * groups * PAD, :] = moved[:, i * LANES : (i + 1) * LANES]
    for g in range(groups):
        lanes = slice(g * LANES, (g + 1) * LANES)

        def lift(p, _):
            total = jnp.zeros((COL, LANES), F32)
            for i in range(ROW):
                line = cells[pl.ds(i * groups * PAD + g * PAD + p, ROW, stride=0), :]
                line = jnp.concatenate([line, line], axis=0)
                total = total + spread_e[i * COL : (i + 1) * COL, lanes] * line
            upper[pl.ds(pl.multiple_of(p * COL, COL), COL), lanes] = total.astype(BF)
            return 0

        lax.fori_loop(0, pairs, lift, 0, unroll=2)

    step = 256
    for n in range(0, next_, step):
        inner = jnp.dot(upper[...], right[:, n : n + step], preferred_element_type=F32)
        out[:, n : n + step] = (inner + diag[:, n : n + step]).astype(BF)

    def drain_rs(t, _):
        swap(t).wait_send()
        scatter(t).wait_send()
        return 0

    lax.fori_loop(0, chips - 1, drain_rs, 0)
    swap(chips - 1).wait_send()
    drain_ao()
    for t in range(nz - 1):
        along(t).wait_send()
    drain_mix()


def residual(offsets, screened, counts, virtuals, amp, integrals, coupling, energies, nz):
    nao, next_ = virtuals.shape
    rows = amp.shape[0]
    pairs = rows // COL
    pieces = pairs // SUB
    nblk = offsets.shape[1]
    groups = nblk // GROUP
    chips = NX * NY
    slots = screened.shape[1]
    vmem = pl.BlockSpec(memory_space=pltpu.VMEM)
    smem = pl.BlockSpec(memory_space=pltpu.SMEM)
    hbm = pl.BlockSpec(memory_space=pltpu.HBM)
    dma = pltpu.SemaphoreType.DMA
    message = (pieces, SUB, WIDTH)
    return pl.pallas_call(
        residual_kernel,
        out_shape=jax.ShapeDtypeStruct((rows, next_), BF),
        in_specs=[smem, smem, smem, hbm, hbm, hbm, vmem, vmem],
        out_specs=vmem,
        scratch_shapes=[
            pltpu.VMEM((nblk * COL, next_), BF),
            pltpu.VMEM((rows, nblk * COL), BF),
            pltpu.VMEM((rows, next_), F32),
            pltpu.VMEM((nao, next_), BF),
            pltpu.VMEM((next_ // LANES, nao, LANES), F32),
            pltpu.VMEM((rows, next_), BF),
            pltpu.VMEM(integrals.shape, BF),
            pltpu.VMEM((GROUP * LANES, GROUP * LANES), BF),
            pltpu.VMEM((groups, rows, LANES), F32),
            pltpu.VMEM((nblk * ROW, LANES), F32),
            pltpu.VMEM((ROW, LANES, nblk), F32),
            pltpu.VMEM((ROW * COL, nblk * COL), F32),
            pltpu.VMEM((groups, COL * ROW, LANES), F32),
            pltpu.VMEM((groups * PAD * ROW, LANES), F32),
            pltpu.VMEM((groups * PAD, ROW * LANES), BF),
            pltpu.VMEM((2, chips, *message), BF),
            pltpu.VMEM((chips, *message), BF),
            pltpu.VMEM((chips, *message), BF),
            pltpu.VMEM((chips, *message), BF),
            pltpu.VMEM(message, BF),
            pltpu.VMEM((2, chips, *message), BF),
            pltpu.VMEM((pairs, slots * WIDTH), F32),
            pltpu.VMEM(message, BF),
            pltpu.VMEM((nz, *message), BF),
            pltpu.VMEM((nz * pairs, WIDTH), F32),
            pltpu.VMEM(message, BF),
            pltpu.VMEM((2, chips, *message), BF),
            dma((-(-nao // VROWS) + 2,)),
            dma((chips,)), dma((chips,)),
            dma((chips,)), dma((chips,)),
            dma((chips,)), dma((chips,)), dma((chips,)), dma((chips,)),
            dma((nz,)), dma((nz,)),
            dma((chips,)), dma((chips,)), dma((chips,)), dma((chips,)),
        ],
        compiler_params=pltpu.CompilerParams(
            collective_id=0, has_side_effects=True, vmem_limit_bytes=58 * 1024 * 1024
        ),
        name="residual",
    )(offsets, screened, counts, virtuals, amp, integrals, coupling, energies)


def shards(amplitudes, virtuals, energies, integrals, screened, counts, offsets, coupling):
    pairs, ext, next_ = amplitudes.shape
    amp = amplitudes.reshape(pairs * ext, next_)
    nz = coupling.shape[1] // pairs
    out = residual(offsets, screened, counts, virtuals, amp, integrals, coupling, energies.reshape(1, next_), nz)
    return out.reshape(pairs, ext, next_)


def solution(mesh):
    return jax.shard_map(
        shards,
        mesh=mesh,
        in_specs=(
            P("pb", "sp", None),
            P(),
            P(),
            P("sp", None),
            P("sp", None),
            P("sp"),
            P(),
            P("pb", None),
        ),
        out_specs=P("pb", "sp", None),
        check_vma=False,
    )
```

time: 69.2 us -> 62 us (0.90)
  Pallas kernels: 68.4 us -> 59.1 us
  local copies, waits for them, and re-layouts: 0 us -> 1.98 us
    pallas_call x3 -> x1, Pallas kernels: 68.4 us -> 59.1 us  [residual(): pl.pallas_call(residual_kernel, out_shape=jax.ShapeDtypeStruct((rows, nex...]
    unnamed x0 -> x1, local copies, waits for them, and re-layouts: none -> 1.98 us
where the time goes in v2:
time: 62 us; the launch traced here: 61.7 us
  Pallas kernels  59.1 us (95%)
  local copies, waits for them, and re-layouts  1.98 us (3%)
  between operations  0.66 us (1%)
    pallas_call x1, Pallas kernels, residual(): pl.pallas_call(residual_kernel, out_shape=jax.ShapeDtypeStruct((rows, nex...  59.1 us
    unnamed x1, local copies, waits for them, and re-layouts  1.98 us

profile of v2, /device:TPU:1, one launch (start us, length us, event | category | flops | bytes accessed | tf_op | source)
XLA Modules:
  0.0 61.7 jit_solution(17748859176210790536)
XLA Ops:
  0.7 59.1 %residual.1 = bf16[320,1024]{1,0:T(8,128)(2,1)} custom-call(s32[2,64]{1,0:T(2,128)} %off.1, s32[1,16]{1,0:T(1,128)} %screened.1, s32[1]{0:T(128)S(6)} %copy.10.counts, bf16[1400,1024]{1,0:T(8,128)(2,1)} %virt.1, bf16[320,1024]{1,0:T(8,128)(2,1)} %bitcast.4, bf16[128,2048]{1,0:T(8,128)(2,1)} %integrals_hbm.1, bf16[20,160]{1,0:T(8,128)(2,1)} %coupling.1, ...), custom_call_target="tpu_custom_call" | custom-call | tf_op jit(solution)/shard_map/residual/pallas_call | solution.py:387
  59.8 2.0 %copy.11 = bf16[20,16,1024]{2,1,0:T(8,128)(2,1)} copy(bf16[20,16,1024]{2,1,0:T(8,128)(2,1)} %bitcast.3) | data formatting | bytes 1310720

commit v3 on v2

--- a/solution.py
+++ b/solution.py
@@ -55,11 +55,6 @@
         dx = far_first(t % NX, NX)
         return ((y + dy) % NY) * NX + (x + dx) % NX
 
-    def source(t):
-        dy = far_first(t // NX, NY)
-        dx = far_first(t % NX, NX)
-        return ((y + NY - dy) % NY) * NX + (x + NX - dx) % NX
-
     barrier = pltpu.get_barrier_semaphore()
 
     def greet(t, _):
@@ -87,7 +82,6 @@
     for load in loads:
         load.start()
     amp_load.start()
-    int_load.start()
 
     def mark(u, _):
         shape = (LANES, GROUP * LANES)
@@ -128,6 +122,7 @@
             spread_a[g, pl.ds(i, COL, stride=ROW), :] = mine[:, g * LANES : (g + 1) * LANES]
 
     amp_load.wait()
+    int_load.start()
     step = 256
     for n in range(0, nblk * COL, step):
         got = lax.dot_general(
@@ -139,11 +134,12 @@
 
     for g in range(groups):
 
+        lefts = [spread_a[g, a * ROW : (a + 1) * ROW, :] for a in range(COL)]
+
         def contract(p, _):
-            total = jnp.zeros((ROW, LANES), F32)
-            for a in range(COL):
-                line = half[g, pl.ds(p * COL + a, ROW, stride=0), :]
-                total = total + spread_a[g, a * ROW : (a + 1) * ROW, :] * line
+            total = lefts[0] * half[g, pl.ds(p * COL, ROW, stride=0), :]
+            for a in range(1, COL):
+                total = total + lefts[a] * half[g, pl.ds(p * COL + a, ROW, stride=0), :]
             cells[pl.ds(pl.multiple_of(g * PAD * ROW + p * ROW, ROW), ROW), :] = total
             return 0
 
@@ -167,45 +163,47 @@
 
     pl.semaphore_wait(barrier, chips + nz - 1)
 
+    def row_to(t):
+        return (y + far_first(t, NY)) % NY
+
+    def row_from(t):
+        return (y + NY - far_first(t, NY)) % NY
+
     def swap(t):
-        to = peer(t)
+        span = pl.ds(row_to(t) * NX, NX)
         return pltpu.make_async_remote_copy(
-            part.at[1 - core, to], pairsum.at[to], pair_s.at[t], pair_r.at[t],
+            part.at[1 - core, span], pairsum.at[span], pair_s, pair_r.at[t],
             device_id=other, device_id_type=MESH,
         )
 
-    def scatter(t):
-        to = peer(t)
-        return pltpu.make_async_remote_copy(
-            outgoing.at[to], arrived.at[chip], rs_s.at[t], rs_r.at[t],
-            device_id=(to * 2 + core, z), device_id_type=MESH,
-        )
-
     def swap_go(t, _):
         swap(t).start()
         return 0
 
-    def pair_total(t):
-        to = peer(t)
+    def scatter_go(t, _):
+        row = row_to(t)
+        span = pl.ds(row * NX, NX)
         swap(t).wait_recv()
-        return part[core, to].astype(F32) + pairsum[to].astype(F32)
-
-    def scatter_go(t, _):
-        outgoing[peer(t)] = pair_total(t).astype(BF)
-        scatter(t).start()
-        return 0
-
-    def scatter_in(t, total):
-        u = chips - 2 - t
-        come = source(u)
-        pltpu.make_async_remote_copy(
-            outgoing.at[come], arrived.at[come], rs_s.at[u], rs_r.at[u],
-            device_id=(come * 2 + core, z), device_id_type=MESH,
-        ).wait_recv()
-        return total + arrived[come].astype(F32)
-
-    lax.fori_loop(0, chips, swap_go, 0)
-    lax.fori_loop(0, chips - 1, scatter_go, 0)
+        outgoing[span] = (part[core, span].astype(F32) + pairsum[span].astype(F32)).astype(BF)
+        for u in range(NX):
+            to = row * NX + (x + far_first(u, NX)) % NX
+
+            @pl.when(t * NX + u < chips - 1)
+            def _():
+                pltpu.make_async_remote_copy(
+                    outgoing.at[to], arrived.at[chip], rs_s, rs_r,
+                    device_id=(to * 2 + core, z), device_id_type=MESH,
+                ).start()
+
+        return 0
+
+    lax.fori_loop(0, NY, swap_go, 0)
+    lax.fori_loop(0, NY, scatter_go, 0)
+
+    most = pl.ds(0, chips - 1)
+    scatter_all = pltpu.make_async_remote_copy(
+        outgoing.at[most], arrived.at[most], rs_s, rs_r, device_id=other, device_id_type=MESH
+    )
 
     def diagonal(p, _):
         at = pl.multiple_of(p * COL, COL)
@@ -213,75 +211,56 @@
         return 0
 
     lax.fori_loop(0, pairs, diagonal, 0)
-    total = lax.fori_loop(0, chips - 1, scatter_in, pair_total(chips - 1))
-    ao_own[...] = total.astype(BF)
+    arrived[chip] = outgoing[chip]
+    scatter_all.wait_recv()
+    ao_own[...] = lax.fori_loop(
+        1, chips, lambda c, total: total + arrived[c].astype(F32), arrived[0].astype(F32), unroll=4
+    ).astype(BF)
 
     def gather(own, landing, send, recv, fsend, frecv):
-        def to_peer(t):
+        def begin(t, _):
+            pltpu.make_async_remote_copy(
+                own, landing.at[core, chip], send, recv.at[t // NX],
+                device_id=(peer(t) * 2 + core, z), device_id_type=MESH,
+            ).start()
+            return 0
+
+        def row_copy(t, side):
+            span = pl.ds(row_from(t) * NX, NX)
             return pltpu.make_async_remote_copy(
-                own, landing.at[core, chip], send.at[t], recv.at[t],
-                device_id=(peer(t) * 2 + core, z), device_id_type=MESH,
-            )
-
-        def from_peer(t):
-            come = source(t)
-            return pltpu.make_async_remote_copy(
-                own, landing.at[core, come], send.at[t], recv.at[t],
-                device_id=(come * 2 + core, z), device_id_type=MESH,
-            )
-
-        def forward(t):
-            come = source(t)
-            return pltpu.make_async_remote_copy(
-                landing.at[core, come], landing.at[core, come], fsend.at[t], frecv.at[t],
+                landing.at[side, span], landing.at[side, span], fsend, frecv,
                 device_id=other, device_id_type=MESH,
             )
 
-        def from_other(t):
-            come = source(t)
+        def come(t, size):
+            span = pl.ds(row_from(t) * NX, size)
             return pltpu.make_async_remote_copy(
-                landing.at[1 - core, come], landing.at[1 - core, come], fsend.at[t], frecv.at[t],
+                landing.at[core, span], landing.at[core, span], send, recv.at[t],
                 device_id=other, device_id_type=MESH,
             )
 
-        def begin(t, _):
-            to_peer(t).start()
+        lax.fori_loop(0, chips - 1, begin, 0)
+        landing[core, chip] = own[...]
+        come(NY - 1, NX - 1).wait_recv()
+        row_copy(NY - 1, core).start()
+
+        def relay(t, _):
+            come(NY - 2 - t, NX).wait_recv()
+            row_copy(NY - 2 - t, core).start()
             return 0
 
-        lax.fori_loop(0, chips - 1, begin, 0)
-        mine = pltpu.make_async_remote_copy(
-            own, landing.at[core, chip], fsend.at[chips - 1], frecv.at[chips - 1],
-            device_id=other, device_id_type=MESH,
+        lax.fori_loop(0, NY - 1, relay, 0)
+        whole = pltpu.make_async_remote_copy(
+            landing.at[core], landing.at[1 - core], fsend, frecv, device_id=other, device_id_type=MESH
         )
-        mine.start()
-        landing[core, chip] = own[...]
-
-        def relay(t, _):
-            u = chips - 2 - t
-            from_peer(u).wait_recv()
-            forward(u).start()
-            return 0
-
-        lax.fori_loop(0, chips - 1, relay, 0)
-        pltpu.make_async_remote_copy(
-            own, landing.at[1 - core, chip], fsend.at[chips - 1], frecv.at[chips - 1],
-            device_id=other, device_id_type=MESH,
-        ).wait_recv()
-
-        def settle(t, _):
-            from_other(chips - 2 - t).wait_recv()
-            return 0
-
-        lax.fori_loop(0, chips - 1, settle, 0)
+        whole.wait_recv()
 
         def drain():
-            def one(t, _):
-                to_peer(t).wait_send()
-                forward(t).wait_send()
-                return 0
-
-            lax.fori_loop(0, chips - 1, one, 0)
-            mine.wait_send()
+            pltpu.make_async_remote_copy(
+                landing.at[core, most], landing.at[core, most], send, recv.at[0],
+                device_id=other, device_id_type=MESH,
+            ).wait_send()
+            whole.wait_send()
 
         return drain
 
@@ -299,24 +278,20 @@
     for j in range(pieces):
         raw_own[j] = raw[j * SUB : (j + 1) * SUB, :].astype(BF)
 
-    def along(t):
-        return pltpu.make_async_remote_copy(
-            raw_own, raw_all.at[z], z_s.at[t], z_r.at[t],
+    def along(t, _):
+        pltpu.make_async_remote_copy(
+            raw_own, raw_all.at[z], z_s, z_r,
             device_id=(sp, (z + far_first(t, nz)) % nz), device_id_type=MESH,
-        )
-
-    def along_in(t):
-        come = (z + nz - far_first(t, nz)) % nz
-        return pltpu.make_async_remote_copy(
-            raw_own, raw_all.at[come], z_s.at[t], z_r.at[t],
-            device_id=(sp, come), device_id_type=MESH,
-        )
-
-    for t in range(nz - 1):
-        along(t).start()
+        ).start()
+        return 0
+
+    lax.fori_loop(0, nz - 1, along, 0)
     raw_all[z] = raw_own[...]
-    for t in range(nz - 1):
-        along_in(t).wait_recv()
+    rest = pl.ds(0, nz - 1)
+    along_all = pltpu.make_async_remote_copy(
+        raw_all.at[rest], raw_all.at[rest], z_s, z_r, device_id=other, device_id_type=MESH
+    )
+    along_all.wait_recv()
     for q in range(nz):
         for j in range(pieces):
             at = q * pairs + j * SUB
@@ -341,12 +316,14 @@
     for g in range(groups):
         lanes = slice(g * LANES, (g + 1) * LANES)
 
+        lefts = [spread_e[i * COL : (i + 1) * COL, lanes] for i in range(ROW)]
+
         def lift(p, _):
-            total = jnp.zeros((COL, LANES), F32)
+            total = None
             for i in range(ROW):
                 line = cells[pl.ds(i * groups * PAD + g * PAD + p, ROW, stride=0), :]
-                line = jnp.concatenate([line, line], axis=0)
-                total = total + spread_e[i * COL : (i + 1) * COL, lanes] * line
+                term = lefts[i] * jnp.concatenate([line, line], axis=0)
+                total = term if total is None else total + term
             upper[pl.ds(pl.multiple_of(p * COL, COL), COL), lanes] = total.astype(BF)
             return 0
 
@@ -357,16 +334,12 @@
         inner = jnp.dot(upper[...], right[:, n : n + step], preferred_element_type=F32)
         out[:, n : n + step] = (inner + diag[:, n : n + step]).astype(BF)
 
-    def drain_rs(t, _):
-        swap(t).wait_send()
-        scatter(t).wait_send()
-        return 0
-
-    lax.fori_loop(0, chips - 1, drain_rs, 0)
-    swap(chips - 1).wait_send()
+    pltpu.make_async_remote_copy(
+        part.at[1 - core], pairsum, pair_s, pair_r.at[0], device_id=other, device_id_type=MESH
+    ).wait_send()
+    scatter_all.wait_send()
     drain_ao()
-    for t in range(nz - 1):
-        along(t).wait_send()
+    along_all.wait_send()
     drain_mix()
 
 
@@ -418,11 +391,11 @@
             pltpu.VMEM(message, BF),
             pltpu.VMEM((2, chips, *message), BF),
             dma((-(-nao // VROWS) + 2,)),
-            dma((chips,)), dma((chips,)),
-            dma((chips,)), dma((chips,)),
-            dma((chips,)), dma((chips,)), dma((chips,)), dma((chips,)),
-            dma((nz,)), dma((nz,)),
-            dma((chips,)), dma((chips,)), dma((chips,)), dma((chips,)),
+            dma, dma((NY,)),
+            dma, dma,
+            dma, dma((NY,)), dma, dma,
+            dma, dma,
+            dma, dma((NY,)), dma, dma,
         ],
         compiler_params=pltpu.CompilerParams(
             collective_id=0, has_side_effects=True, vmem_limit_bytes=58 * 1024 * 1024

time: 62 us -> 56.8 us (0.916)
  Pallas kernels: 59.1 us -> 53.9 us
    pallas_call x1, Pallas kernels: 59.1 us -> 53.9 us  [residual(): pl.pallas_call(residual_kernel, out_shape=jax.ShapeDtypeStruct((rows, nex...]
where the time goes in v3:
time: 56.8 us; the launch traced here: 56.6 us
  Pallas kernels  53.9 us (95%)
  local copies, waits for them, and re-layouts  1.98 us (3%)
  between operations  0.66 us (1%)
    pallas_call x1, Pallas kernels, residual(): pl.pallas_call(residual_kernel, out_shape=jax.ShapeDtypeStruct((rows, nex...  53.9 us
    unnamed x1, local copies, waits for them, and re-layouts  1.98 us

profile of v3, /device:TPU:1, one launch (start us, length us, event | category | flops | bytes accessed | tf_op | source)
XLA Modules:
  0.0 56.6 jit_solution(12451956438222561293)
XLA Ops:
  0.7 53.9 %residual.1 = bf16[320,1024]{1,0:T(8,128)(2,1)} custom-call(s32[2,64]{1,0:T(2,128)} %off.1, s32[1,16]{1,0:T(1,128)} %screened.1, s32[1]{0:T(128)S(6)} %copy.10.counts, bf16[1400,1024]{1,0:T(8,128)(2,1)} %virt.1, bf16[320,1024]{1,0:T(8,128)(2,1)} %bitcast.4, bf16[128,2048]{1,0:T(8,128)(2,1)} %integrals_hbm.1, bf16[20,160]{1,0:T(8,128)(2,1)} %coupling.1, ...), custom_call_target="tpu_custom_call" | custom-call | tf_op jit(solution)/shard_map/residual/pallas_call | solution.py:360
  54.6 2.0 %copy.11 = bf16[20,16,1024]{2,1,0:T(8,128)(2,1)} copy(bf16[20,16,1024]{2,1,0:T(8,128)(2,1)} %bitcast.3) | data formatting | bytes 1310720

commit v4 on v3

--- a/solution.py
+++ b/solution.py
@@ -19,6 +19,7 @@
 PAD = 24
 VROWS = 176
 NX, NY = 4, 8
+BOTH = 4
 
 
 def far_first(t, size):
@@ -26,8 +27,8 @@
 
 
 def residual_kernel(
-    off, screened, counts, virt, amp_hbm, integrals_hbm, coupling, energies, out,
-    right, upper, diag, vbuf, vf, amp, integrals, perm, half, lrows, lt, spread_e, spread_a, cells, stacked,
+    off, screened, counts, virt, amp_hbm, integrals_hbm, coupling_hbm, energies_hbm, out_hbm,
+    right, upper, diag, out, coupling, energies, vbuf, vf, amp, integrals, perm, half, lrows, lt, spread_e, spread_a, cells, stacked,
     part, pairsum, outgoing, arrived, ao_own, ao_all, chosen, raw_own, raw_all, raw_rows, mix_own, mixed_all,
     local_s, pair_s, pair_r, rs_s, rs_r, ag_s, ag_r, fw_s, fw_r, z_s, z_r, mg_s, mg_r, mf_s, mf_r,
 ):
@@ -50,25 +51,15 @@
     y = chip // NX
     other = (chip * 2 + (1 - core), z)
 
-    def peer(t):
-        dy = far_first(t // NX, NY)
-        dx = far_first(t % NX, NX)
-        return ((y + dy) % NY) * NX + (x + dx) % NX
-
-    barrier = pltpu.get_barrier_semaphore()
-
-    def greet(t, _):
-        pl.semaphore_signal(barrier, inc=1, device_id=(peer(t) * 2 + core, z), device_id_type=MESH)
-        return 0
-
-    lax.fori_loop(0, chips - 1, greet, 0)
-
-    def greet_z(t, _):
-        pl.semaphore_signal(barrier, inc=1, device_id=(sp, (z + 1 + t) % nz), device_id_type=MESH)
-        return 0
-
-    lax.fori_loop(0, nz - 1, greet_z, 0)
-    pl.semaphore_signal(barrier, inc=1, device_id=other, device_id_type=MESH)
+    row_list = [lax.rem(y + far_first(t, NY), NY) for t in range(NY)]
+    col_list = [lax.rem(x + far_first(u, NX), NX) for u in range(NX)]
+    row_chip = [row * NX for row in row_list]
+    row_core = [first * 2 + core for first in row_chip]
+    col_core = [col * 2 for col in col_list]
+    peers = [(t, u) for t in range(NY) for u in range(NX)][:-1]
+
+    def member(t, u):
+        return (row_core[t] + col_core[u], z)
 
     starts = list(range(0, nao, VROWS))
     loads = []
@@ -79,9 +70,19 @@
         )
     amp_load = pltpu.make_async_copy(amp_hbm, amp, local_s.at[len(starts)])
     int_load = pltpu.make_async_copy(integrals_hbm, integrals, local_s.at[len(starts) + 1])
+    coupling_load = pltpu.make_async_copy(coupling_hbm, coupling, local_s.at[len(starts) + 2])
+    energy_load = pltpu.make_async_copy(energies_hbm, energies, local_s.at[len(starts) + 3])
     for load in loads:
         load.start()
     amp_load.start()
+
+    barrier = pltpu.get_barrier_semaphore()
+    for t, u in peers:
+        pl.semaphore_signal(barrier, inc=1, device_id=member(t, u), device_id_type=MESH)
+    z_list = [lax.rem(z + far_first(t, nz), nz) for t in range(nz)]
+    for t in range(nz - 1):
+        pl.semaphore_signal(barrier, inc=1, device_id=(sp, z_list[t]), device_id_type=MESH)
+    pl.semaphore_signal(barrier, inc=1, device_id=other, device_id_type=MESH)
 
     def mark(u, _):
         shape = (LANES, GROUP * LANES)
@@ -103,14 +104,18 @@
     tile0 = sp * COL // LANES
     sub0 = pl.multiple_of((sp * COL) % LANES, COL)
 
-    def pick(b, _):
-        to = pl.multiple_of(b * COL, COL)
-        for t in range(tiles):
-            right[pl.ds(to, COL), t * LANES : (t + 1) * LANES] = vf[t, pl.ds(off[1, b], COL), :].astype(BF)
-        lrows[pl.ds(pl.multiple_of(b * ROW, ROW), ROW), :] = vf[tile0, pl.ds(off[0, b], ROW), :]
-        return 0
-
-    lax.fori_loop(0, nblk, pick, 0, unroll=2)
+    for g in range(groups):
+
+        def pick(j, _):
+            owner = row_list[g] * GROUP + j
+            to = pl.multiple_of(g * LANES + j * COL, COL)
+            for t in range(tiles):
+                right[pl.ds(to, COL), t * LANES : (t + 1) * LANES] = vf[t, pl.ds(off[1, owner], COL), :].astype(BF)
+            at = pl.multiple_of((g * GROUP + j) * ROW, ROW)
+            lrows[pl.ds(at, ROW), :] = vf[tile0, pl.ds(off[0, owner], ROW), :]
+            return 0
+
+        lax.fori_loop(0, GROUP, pick, 0, unroll=2)
 
     owner = lax.broadcasted_iota(jnp.int32, (nblk, nblk * COL), 1) // COL
     repeat = jnp.where(lax.broadcasted_iota(jnp.int32, (nblk, nblk * COL), 0) == owner, 1.0, 0.0).astype(BF)
@@ -123,87 +128,83 @@
 
     amp_load.wait()
     int_load.start()
-    step = 256
-    for n in range(0, nblk * COL, step):
-        got = lax.dot_general(
-            amp[...], right[n : n + step, :], (((1,), (1,)), ((), ())), preferred_element_type=F32
+    coupling_load.start()
+    energy_load.start()
+
+    def swap(t):
+        span = pl.ds(row_chip[t], NX)
+        return pltpu.make_async_remote_copy(
+            part.at[1 - core, span], pairsum.at[span], pair_s, pair_r.at[t],
+            device_id=other, device_id_type=MESH,
         )
-        got = got.astype(BF).astype(F32)
-        for t in range(step // LANES):
-            half[n // LANES + t] = got[:, t * LANES : (t + 1) * LANES]
-
-    for g in range(groups):
-
-        lefts = [spread_a[g, a * ROW : (a + 1) * ROW, :] for a in range(COL)]
-
-        def contract(p, _):
-            total = lefts[0] * half[g, pl.ds(p * COL, ROW, stride=0), :]
-            for a in range(1, COL):
-                total = total + lefts[a] * half[g, pl.ds(p * COL + a, ROW, stride=0), :]
-            cells[pl.ds(pl.multiple_of(g * PAD * ROW + p * ROW, ROW), ROW), :] = total
-            return 0
-
-        lax.fori_loop(0, pairs, contract, 0, unroll=2)
-        for i in range(ROW):
-            stacked[g * PAD : (g + 1) * PAD, i * LANES : (i + 1) * LANES] = cells[
-                pl.ds(g * PAD * ROW + i, PAD, stride=ROW), :
-            ].astype(BF)
-    moved = jnp.dot(stacked[...], perm[...], preferred_element_type=F32)
-    for g in range(groups):
-        for v in range(GROUP):
-            for j in range(pieces):
-                part[v % 2, (g * GROUP + v) // 2, j] = moved[
-                    g * PAD + j * SUB : g * PAD + (j + 1) * SUB, v * LANES : (v + 1) * LANES
+
+    def scatter(t):
+        span = pl.ds(row_chip[t], NX)
+        swap(t).wait_recv()
+        outgoing[span] = (part[core, span].astype(F32) + pairsum[span].astype(F32)).astype(BF)
+        for u in range(NX):
+            if (t, u) in peers:
+                pltpu.make_async_remote_copy(
+                    outgoing.at[row_chip[t] + col_list[u]], arrived.at[chip], rs_s, rs_r,
+                    device_id=member(t, u), device_id_type=MESH,
+                ).start()
+
+    both = BOTH
+    steps = NY // both
+    step = both * LANES
+    wide = 2 * LANES
+    for k in range(steps):
+        for n in range(k * step, (k + 1) * step, wide):
+            got = lax.dot_general(
+                amp[...], right[n : n + wide, :], (((1,), (1,)), ((), ())), preferred_element_type=F32
+            )
+            got = got.astype(BF).astype(F32)
+            for t in range(wide // LANES):
+                half[n // LANES + t] = got[:, t * LANES : (t + 1) * LANES]
+        for g in range(k * both, (k + 1) * both):
+            lefts = [spread_a[g, a * ROW : (a + 1) * ROW, :] for a in range(COL)]
+
+            def contract(p, _):
+                total = lefts[0] * half[g, pl.ds(p * COL, ROW, stride=0), :]
+                for a in range(1, COL):
+                    total = total + lefts[a] * half[g, pl.ds(p * COL + a, ROW, stride=0), :]
+                cells[pl.ds(pl.multiple_of(g * PAD * ROW + p * ROW, ROW), ROW), :] = total
+                return 0
+
+            lax.fori_loop(0, pairs, contract, 0, unroll=4)
+            for i in range(ROW):
+                stacked[g * PAD : (g + 1) * PAD, i * LANES : (i + 1) * LANES] = cells[
+                    pl.ds(g * PAD * ROW + i, PAD, stride=ROW), :
                 ].astype(BF)
-
+        moved = jnp.dot(
+            stacked[k * both * PAD : (k + 1) * both * PAD, :], perm[...], preferred_element_type=F32
+        )
+        for g in range(both):
+            for v in range(GROUP):
+                for j in range(pieces):
+                    part[v % 2, row_chip[k * both + g] + v // 2, j] = moved[
+                        g * PAD + j * SUB : g * PAD + (j + 1) * SUB, v * LANES : (v + 1) * LANES
+                    ].astype(BF)
+        if k == 0:
+            pl.semaphore_wait(barrier, chips + nz - 1)
+        for t in range(k * both, (k + 1) * both):
+            swap(t).start()
+        if k > 0:
+            for t in range((k - 1) * both, k * both):
+                scatter(t)
+    for t in range((steps - 1) * both, steps * both):
+        scatter(t)
+
+    most = pl.ds(0, chips - 1)
+    scatter_all = pltpu.make_async_remote_copy(
+        outgoing.at[most], arrived.at[most], rs_s, rs_r, device_id=other, device_id_type=MESH
+    )
+
+    energy_load.wait()
     hit = lax.broadcasted_iota(jnp.int32, (COL, next_), 1) == (
         lax.broadcasted_iota(jnp.int32, (COL, next_), 0) + sp * COL
     )
     own_energy = jnp.sum(jnp.where(hit, energies[...], 0.0), axis=1, keepdims=True)
-
-    pl.semaphore_wait(barrier, chips + nz - 1)
-
-    def row_to(t):
-        return (y + far_first(t, NY)) % NY
-
-    def row_from(t):
-        return (y + NY - far_first(t, NY)) % NY
-
-    def swap(t):
-        span = pl.ds(row_to(t) * NX, NX)
-        return pltpu.make_async_remote_copy(
-            part.at[1 - core, span], pairsum.at[span], pair_s, pair_r.at[t],
-            device_id=other, device_id_type=MESH,
-        )
-
-    def swap_go(t, _):
-        swap(t).start()
-        return 0
-
-    def scatter_go(t, _):
-        row = row_to(t)
-        span = pl.ds(row * NX, NX)
-        swap(t).wait_recv()
-        outgoing[span] = (part[core, span].astype(F32) + pairsum[span].astype(F32)).astype(BF)
-        for u in range(NX):
-            to = row * NX + (x + far_first(u, NX)) % NX
-
-            @pl.when(t * NX + u < chips - 1)
-            def _():
-                pltpu.make_async_remote_copy(
-                    outgoing.at[to], arrived.at[chip], rs_s, rs_r,
-                    device_id=(to * 2 + core, z), device_id_type=MESH,
-                ).start()
-
-        return 0
-
-    lax.fori_loop(0, NY, swap_go, 0)
-    lax.fori_loop(0, NY, scatter_go, 0)
-
-    most = pl.ds(0, chips - 1)
-    scatter_all = pltpu.make_async_remote_copy(
-        outgoing.at[most], arrived.at[most], rs_s, rs_r, device_id=other, device_id_type=MESH
-    )
 
     def diagonal(p, _):
         at = pl.multiple_of(p * COL, COL)
@@ -218,38 +219,32 @@
     ).astype(BF)
 
     def gather(own, landing, send, recv, fsend, frecv):
-        def begin(t, _):
-            pltpu.make_async_remote_copy(
-                own, landing.at[core, chip], send, recv.at[t // NX],
-                device_id=(peer(t) * 2 + core, z), device_id_type=MESH,
-            ).start()
-            return 0
-
-        def row_copy(t, side):
-            span = pl.ds(row_from(t) * NX, NX)
+        def come(t, size):
+            span = pl.ds(row_chip[t], size)
             return pltpu.make_async_remote_copy(
-                landing.at[side, span], landing.at[side, span], fsend, frecv,
+                landing.at[core, span], landing.at[core, span], send, recv.at[row_list[t]],
                 device_id=other, device_id_type=MESH,
             )
 
-        def come(t, size):
-            span = pl.ds(row_from(t) * NX, size)
+        def forward(t):
+            span = pl.ds(row_chip[t], NX)
             return pltpu.make_async_remote_copy(
-                landing.at[core, span], landing.at[core, span], send, recv.at[t],
+                landing.at[core, span], landing.at[core, span], fsend, frecv,
                 device_id=other, device_id_type=MESH,
             )
 
-        lax.fori_loop(0, chips - 1, begin, 0)
+        for t, u in peers:
+            pltpu.make_async_remote_copy(
+                own, landing.at[core, chip], send, recv.at[y],
+                device_id=member(t, u), device_id_type=MESH,
+            ).start()
         landing[core, chip] = own[...]
         come(NY - 1, NX - 1).wait_recv()
-        row_copy(NY - 1, core).start()
-
-        def relay(t, _):
-            come(NY - 2 - t, NX).wait_recv()
-            row_copy(NY - 2 - t, core).start()
-            return 0
-
-        lax.fori_loop(0, NY - 1, relay, 0)
+        forward(NY - 1).start()
+
+        for t in reversed(range(NY - 1)):
+            come(t, NX).wait_recv()
+            forward(t).start()
         whole = pltpu.make_async_remote_copy(
             landing.at[core], landing.at[1 - core], fsend, frecv, device_id=other, device_id_type=MESH
         )
@@ -278,14 +273,10 @@
     for j in range(pieces):
         raw_own[j] = raw[j * SUB : (j + 1) * SUB, :].astype(BF)
 
-    def along(t, _):
+    for t in range(nz - 1):
         pltpu.make_async_remote_copy(
-            raw_own, raw_all.at[z], z_s, z_r,
-            device_id=(sp, (z + far_first(t, nz)) % nz), device_id_type=MESH,
+            raw_own, raw_all.at[z], z_s, z_r, device_id=(sp, z_list[t]), device_id_type=MESH
         ).start()
-        return 0
-
-    lax.fori_loop(0, nz - 1, along, 0)
     raw_all[z] = raw_own[...]
     rest = pl.ds(0, nz - 1)
     along_all = pltpu.make_async_remote_copy(
@@ -296,6 +287,7 @@
         for j in range(pieces):
             at = q * pairs + j * SUB
             raw_rows[at : at + SUB, :] = raw_all[q, j].astype(F32)
+    coupling_load.wait()
     mix = jnp.dot(coupling[...], raw_rows[...].astype(BF), preferred_element_type=F32)
     for j in range(pieces):
         mix_own[j] = mix[j * SUB : (j + 1) * SUB, :].astype(BF)
@@ -303,7 +295,7 @@
     drain_mix = gather(mix_own, mixed_all, mg_s, mg_r, mf_s, mf_r)
 
     for b in range(nblk):
-        block = mixed_all[b % 2, b // 2].astype(F32)
+        block = mixed_all[b % 2, row_chip[b // GROUP] + (b % GROUP) // 2].astype(F32)
         for j in range(pieces):
             cells[b * PAD + j * SUB : b * PAD + (j + 1) * SUB, :] = block[j]
     for g in range(groups):
@@ -329,10 +321,19 @@
 
         lax.fori_loop(0, pairs, lift, 0, unroll=2)
 
-    step = 256
-    for n in range(0, next_, step):
-        inner = jnp.dot(upper[...], right[:, n : n + step], preferred_element_type=F32)
-        out[:, n : n + step] = (inner + diag[:, n : n + step]).astype(BF)
+    stores = []
+    for n in range(0, next_, wide):
+        span = slice(n, n + wide)
+        total = diag[:, span] + jnp.dot(upper[...], right[:, span], preferred_element_type=F32)
+        out[:, span] = total.astype(BF)
+        stores.append(
+            pltpu.make_async_copy(
+                out.at[:, pl.ds(n, wide)], out_hbm.at[:, pl.ds(n, wide)], local_s.at[n // wide]
+            )
+        )
+        stores[-1].start()
+    for store in stores:
+        store.wait()
 
     pltpu.make_async_remote_copy(
         part.at[1 - core], pairsum, pair_s, pair_r.at[0], device_id=other, device_id_type=MESH
@@ -352,7 +353,6 @@
     groups = nblk // GROUP
     chips = NX * NY
     slots = screened.shape[1]
-    vmem = pl.BlockSpec(memory_space=pltpu.VMEM)
     smem = pl.BlockSpec(memory_space=pltpu.SMEM)
     hbm = pl.BlockSpec(memory_space=pltpu.HBM)
     dma = pltpu.SemaphoreType.DMA
@@ -360,12 +360,15 @@
     return pl.pallas_call(
         residual_kernel,
         out_shape=jax.ShapeDtypeStruct((rows, next_), BF),
-        in_specs=[smem, smem, smem, hbm, hbm, hbm, vmem, vmem],
-        out_specs=vmem,
+        in_specs=[smem, smem, smem, hbm, hbm, hbm, hbm, hbm],
+        out_specs=hbm,
         scratch_shapes=[
             pltpu.VMEM((nblk * COL, next_), BF),
             pltpu.VMEM((rows, nblk * COL), BF),
             pltpu.VMEM((rows, next_), F32),
+            pltpu.VMEM((rows, next_), BF),
+            pltpu.VMEM(coupling.shape, BF),
+            pltpu.VMEM(energies.shape, F32),
             pltpu.VMEM((nao, next_), BF),
             pltpu.VMEM((next_ // LANES, nao, LANES), F32),
             pltpu.VMEM((rows, next_), BF),
@@ -390,7 +393,7 @@
             pltpu.VMEM((nz * pairs, WIDTH), F32),
             pltpu.VMEM(message, BF),
             pltpu.VMEM((2, chips, *message), BF),
-            dma((-(-nao // VROWS) + 2,)),
+            dma((-(-nao // VROWS) + 4,)),
             dma, dma((NY,)),
             dma, dma,
             dma, dma((NY,)), dma, dma,

time: 56.8 us -> 53.4 us (0.940)
  Pallas kernels: 53.9 us -> 50.6 us
    pallas_call x1, Pallas kernels: 53.9 us -> 50.6 us  [residual(): pl.pallas_call(residual_kernel, out_shape=jax.ShapeDtypeStruct((rows, nex...]
where the time goes in v4:
time: 53.4 us; the launch traced here: 53.2 us
  Pallas kernels  50.6 us (95%)
  local copies, waits for them, and re-layouts  1.98 us (4%)
  between operations  0.66 us (1%)
    pallas_call x1, Pallas kernels, residual(): pl.pallas_call(residual_kernel, out_shape=jax.ShapeDtypeStruct((rows, nex...  50.6 us
    unnamed x1, local copies, waits for them, and re-layouts  1.98 us

profile of v4, /device:TPU:1, one launch (start us, length us, event | category | flops | bytes accessed | tf_op | source)
XLA Modules:
  0.0 53.2 jit_solution(9129316686178640816)
XLA Ops:
  0.7 50.6 %residual.1 = bf16[320,1024]{1,0:T(8,128)(2,1)} custom-call(s32[2,64]{1,0:T(2,128)} %off.1, s32[1,16]{1,0:T(1,128)} %screened.1, s32[1]{0:T(128)S(6)} %copy.10.counts, bf16[1400,1024]{1,0:T(8,128)(2,1)} %virt.1, bf16[320,1024]{1,0:T(8,128)(2,1)} %bitcast.4, bf16[128,2048]{1,0:T(8,128)(2,1)} %integrals_hbm.1, bf16[20,160]{1,0:T(8,128)(2,1)} %coupling_hbm.1, ...), custom_call_target="tpu_custom_call" | custom-call | tf_op jit(solution)/shard_map/residual/pallas_call | solution.py:360
  51.2 2.0 %copy.11 = bf16[20,16,1024]{2,1,0:T(8,128)(2,1)} copy(bf16[20,16,1024]{2,1,0:T(8,128)(2,1)} %bitcast.3) | data formatting | bytes 1310720

commit v5 on v4

--- a/solution.py
+++ b/solution.py
@@ -58,6 +58,12 @@
     col_core = [col * 2 for col in col_list]
     peers = [(t, u) for t in range(NY) for u in range(NX)][:-1]
 
+    def hops(pair):
+        dy, dx = far_first(pair[0], NY), far_first(pair[1], NX)
+        return min(dy, NY - dy) + min(dx, NX - dx)
+
+    by_hops = sorted(peers, key=lambda pair: -hops(pair))
+
     def member(t, u):
         return (row_core[t] + col_core[u], z)
 
@@ -115,7 +121,7 @@
             lrows[pl.ds(at, ROW), :] = vf[tile0, pl.ds(off[0, owner], ROW), :]
             return 0
 
-        lax.fori_loop(0, GROUP, pick, 0, unroll=2)
+        lax.fori_loop(0, GROUP, pick, 0, unroll=4)
 
     owner = lax.broadcasted_iota(jnp.int32, (nblk, nblk * COL), 1) // COL
     repeat = jnp.where(lax.broadcasted_iota(jnp.int32, (nblk, nblk * COL), 0) == owner, 1.0, 0.0).astype(BF)
@@ -233,7 +239,7 @@
                 device_id=other, device_id_type=MESH,
             )
 
-        for t, u in peers:
+        for t, u in by_hops:
             pltpu.make_async_remote_copy(
                 own, landing.at[core, chip], send, recv.at[y],
                 device_id=member(t, u), device_id_type=MESH,
@@ -319,7 +325,7 @@
             upper[pl.ds(pl.multiple_of(p * COL, COL), COL), lanes] = total.astype(BF)
             return 0
 
-        lax.fori_loop(0, pairs, lift, 0, unroll=2)
+        lax.fori_loop(0, pairs, lift, 0, unroll=4)
 
     stores = []
     for n in range(0, next_, wide):

time: 53.4 us -> 53.2 us (level)
  no operation moved by 1% of the time
where the time goes in v5:
time: 53.2 us; the launch traced here: 52.9 us
  Pallas kernels  50.3 us (95%)
  local copies, waits for them, and re-layouts  1.98 us (4%)
  between operations  0.66 us (1%)
    pallas_call x1, Pallas kernels, residual(): pl.pallas_call(residual_kernel, out_shape=jax.ShapeDtypeStruct((rows, nex...  50.3 us
    unnamed x1, local copies, waits for them, and re-layouts  1.98 us

profile of v5, /device:TPU:1, one launch (start us, length us, event | category | flops | bytes accessed | tf_op | source)
XLA Modules:
  0.0 52.9 jit_solution(9035153656351255945)
XLA Ops:
  0.7 50.3 %residual.1 = bf16[320,1024]{1,0:T(8,128)(2,1)} custom-call(s32[2,64]{1,0:T(2,128)} %off.1, s32[1,16]{1,0:T(1,128)} %screened.1, s32[1]{0:T(128)S(6)} %copy.10.counts, bf16[1400,1024]{1,0:T(8,128)(2,1)} %virt.1, bf16[320,1024]{1,0:T(8,128)(2,1)} %bitcast.4, bf16[128,2048]{1,0:T(8,128)(2,1)} %integrals_hbm.1, bf16[20,160]{1,0:T(8,128)(2,1)} %coupling_hbm.1, ...), custom_call_target="tpu_custom_call" | custom-call | tf_op jit(solution)/shard_map/residual/pallas_call | solution.py:366
  51.0 2.0 %copy.11 = bf16[20,16,1024]{2,1,0:T(8,128)(2,1)} copy(bf16[20,16,1024]{2,1,0:T(8,128)(2,1)} %bitcast.3) | data formatting | bytes 1310720
